TPU v7x, 32 devices: a whole 2x2x4 slice. The times are simulated.
32 devices in a mesh: gx: 4 (over x, core), gy: 2 (over y), gz: 4 (over z).
Axes of the slice: x: 2, y: 2, z: 4, core: 2. Of those that a mesh axis runs over, the one named last changes fastest.
Arguments:
- solution: float32 [16, 8, 16, 256], P(None, 'gx', 'gz', 'gy'), may hold values from -0.6 to 0.6
- residual: float32 [16, 8, 16, 256], P(None, 'gx', 'gz', 'gy'), may hold values from -6 to 6
- direction_prev: float32 [16, 8, 16, 256], P(None, 'gx', 'gz', 'gy'), may hold values from -0.3 to 0.3, as said below
- image_prev: float32 [16, 8, 16, 256], P(None, 'gx', 'gz', 'gy'), may hold values from -9 to 9, as said below
- gram_prev: float32 [16, 16], replicated, may hold values from -32768 to 32768, as said below
Outputs:
- solution_new: float32 [16, 8, 16, 256], P(None, 'gx', 'gz', 'gy')
- residual_new: float32 [16, 8, 16, 256], P(None, 'gx', 'gz', 'gy')
- direction: float32 [16, 8, 16, 256], P(None, 'gx', 'gz', 'gy')
Inputs may be any that keep to these rules, and one draw needn't show every extreme that they name: direction_prev is a field of order 0.05. image_prev equals A direction_prev, computed in float32. gram_prev is symmetric and positive definite.
All inputs are finite; a program needn't handle non-finite values.
Results may differ from a plain program's by a relative error of at most 0.0001.
Values sent between devices are 32-bit elements; how exact they have to be, the bound alone decides.
A program may use at most 64 MiB of HBM per device.

v0:
```python
import functools

import jax
import jax.numpy as jnp
from jax import lax
from jax.experimental import pallas as pl
from jax.experimental.pallas import tpu as pltpu
from jax.sharding import PartitionSpec as P


def with_halo(value, sides, width):
    for axis, dim in sides:
        devices, length = (lax.axis_size(axis), value.shape[dim])
        up = [(i, (i + 1) % devices) for i in range(devices - 1)]
        down = [(j, i) for i, j in up]
        last = lax.slice_in_dim(value, length - width, length, axis=dim)
        first = lax.slice_in_dim(value, 0, width, axis=dim)
        before = lax.ppermute(last, axis, up)
        after = lax.ppermute(first, axis, down)
        value = jnp.concatenate([before, value, after], axis=dim)
    return value


def box_sum(padded):
    total = padded[:, :-2] + padded[:, 1:-1] + padded[:, 2:]
    total = total[:, :, :-2] + total[:, :, 1:-1] + total[:, :, 2:]
    return total[:, :, :, :-2] + total[:, :, :, 1:-1] + total[:, :, :, 2:]


def colors_of(shape):
    first = lax.broadcasted_iota(jnp.int32, shape, 1) % 2
    second = lax.broadcasted_iota(jnp.int32, shape, 2) % 2
    third = lax.broadcasted_iota(jnp.int32, shape, 3) % 2
    return 4 * first + 2 * second + third


def local_gram(left, right):
    return jnp.einsum("kxzy,lxzy->kl", left, right, precision=lax.Precision.HIGHEST)


def combine(field, mixing):
    return jnp.einsum("kxzy,kl->lxzy", field, mixing, precision=lax.Precision.HIGHEST)


def small_dot(left, right):
    return jnp.dot(left, right, precision=lax.Precision.HIGHEST)


def spd_solve(matrix, target):
    order = matrix.shape[0]
    sym = 0.5 * (matrix + matrix.T)
    lower = jnp.zeros_like(sym)
    for col in range(order):
        column = sym[col:, col] - jnp.sum(lower[col:, :col] * lower[col, :col][None, :], axis=1)
        pivot = jnp.sqrt(column[0])
        lower = lower.at[col:, col].set(column / pivot)
    middle = jnp.zeros_like(target)
    for row in range(order):
        value = target[row] - jnp.sum(lower[row, :row][:, None] * middle[:row], axis=0)
        middle = middle.at[row].set(value / lower[row, row])
    answer = jnp.zeros_like(target)
    for row in range(order - 1, -1, -1):
        value = middle[row] - jnp.sum(lower[row + 1 :, row][:, None] * answer[row + 1 :], axis=0)
        answer = answer.at[row].set(value / lower[row, row])
    return answer


def sweep_box(field):
    padded = with_halo(field, (("gx", 1), ("gy", 3), ("gz", 2)), 1)
    return box_sum(padded)


def body(solution, residual, direction_prev, image_prev, gram_prev):
    colors = colors_of(residual.shape)
    smoothed = jnp.where(colors == 0, residual / 26.0, jnp.float32(0.0))
    for shade in list(range(1, 8)) + list(range(6, -1, -1)):
        boxed = sweep_box(smoothed)
        smoothed = jnp.where(colors == shade, (residual + boxed - smoothed) / 26.0, smoothed)
    padded = with_halo(smoothed, (("gx", 1), ("gy", 3), ("gz", 2)), 1)
    image = 27.0 * smoothed - box_sum(padded)
    sums = (
        local_gram(smoothed, residual),
        local_gram(smoothed, image),
        local_gram(smoothed, image_prev),
        local_gram(direction_prev, image),
        local_gram(direction_prev, image_prev),
    )
    gram_zr, gram_zw, gram_zq, gram_pw, gram_pq = lax.psum(
        (sums[0], sums[1], sums[2], sums[3], sums[4]), ("gx", "gy", "gz")
    )
    beta_mix = spd_solve(gram_prev, gram_zr)
    direction = smoothed + combine(direction_prev, beta_mix)
    image_new = image + combine(image_prev, beta_mix)
    curvature = gram_zw + small_dot(gram_zq, beta_mix) + small_dot(beta_mix.T, gram_pw)
    curvature = curvature + small_dot(small_dot(beta_mix.T, gram_pq), beta_mix)
    alpha_step = spd_solve(curvature, gram_zr)
    solution_new = solution + combine(direction, alpha_step)
    residual_new = residual - combine(image_new, alpha_step)
    return (solution_new, residual_new, direction)


MESH = pl.DeviceIdType.MESH
HIGHEST = lax.Precision.HIGHEST


def dot(left, right):
    return jnp.dot(left, right, precision=HIGHEST, preferred_element_type=jnp.float32)


def dot_nt(left, right):
    return lax.dot_general(
        left, right, (((1,), (1,)), ((), ())), precision=HIGHEST, preferred_element_type=jnp.float32
    )


def eliminate(matrix, target):
    matrix = 0.5 * (matrix + matrix.T)
    order = matrix.shape[0]
    rows = lax.broadcasted_iota(jnp.int32, matrix.shape, 0)
    for c in range(order):
        column = jnp.broadcast_to(matrix[:, c : c + 1], matrix.shape)
        scale = 1.0 / column[c : c + 1, :]
        mrow = matrix[c : c + 1, :] * scale
        trow = target[c : c + 1, :] * scale
        here = rows == c
        target = jnp.where(here, trow, target - column * trow)
        if c < order - 1:
            matrix = jnp.where(here, mrow, matrix - column * mrow)
    return target


def smooth(res, ngx, ngz, gy, width):
    lx, lz = len(res), len(res[0])
    count, ny = res[0][0].shape
    row = lax.broadcasted_iota(jnp.int32, (count, ny), 0)
    lane = lax.broadcasted_iota(jnp.int32, (count, ny), 1)
    even = lane % 2 == 0
    edges = {
        "xp": (row < ngz, ngz, 0),
        "xn": (row >= count - ngz, count - ngz, 0),
        "zp": (row % ngz == 0, 1, 0),
        "zn": (row % ngz == ngz - 1, count - 1, 0),
        "yp": (lane == jnp.where(gy == 0, 0, -1), 1, 1),
        "yn": (lane == jnp.where(gy == 0, -1, width - 1), ny - 1, 1),
    }
    zero = jnp.zeros((count, ny), jnp.float32)
    memo = {}

    def moved(value, kind):
        if value is None:
            return None
        key = (kind, id(value))
        if key not in memo:
            edge, amount, axis = edges[kind]
            memo[key] = (value, jnp.where(edge, zero, pltpu.roll(value, amount, axis)))
        return memo[key][1]

    def add(*values):
        total = None
        for value in values:
            if value is not None:
                total = value if total is None else total + value
        return total

    state = {(x, z): None for x in range(lx) for z in range(lz)}

    def z_pair(x, z):
        before = state[x, z - 1] if z > 0 else moved(state[x, lz - 1], "zp")
        after = state[x, z + 1] if z < lz - 1 else moved(state[x, 0], "zn")
        return add(before, after)

    def neighbours(x, z):
        def line(other):
            return add(state[other, z], z_pair(other, z))

        before = line(x - 1) if x > 0 else moved_line(lx - 1, z, "xp")
        after = line(x + 1) if x < lx - 1 else moved_line(0, z, "xn")
        return add(z_pair(x, z), before, after)

    def moved_line(x, z, kind):
        return moved(add(state[x, z], z_pair(x, z)), kind)

    def y_pair(value):
        return moved(value, "yp") + moved(value, "yn")

    third = jnp.float32(1.0 / 26.0)
    plan = [(0, 0, (0, 1)), (0, 1, (0, 1)), (1, 0, (0, 1)), (1, 1, (0, 1, 0)), (1, 0, (1, 0)), (0, 1, (1, 0)), (0, 0, (1, 0))]
    for xp, zp, shades in plan:
        fresh = {}
        for x in range(xp, lx, 2):
            for z in range(zp, lz, 2):
                near = neighbours(x, z)
                base = res[x][z] if near is None else res[x][z] + (near + y_pair(near))
                value = state[x, z]
                for shade in shades:
                    total = base if value is None else base + y_pair(value)
                    chosen = even if shade == 0 else jnp.logical_not(even)
                    value = jnp.where(chosen, total * third, zero if value is None else value)
                fresh[x, z] = value
        state.update(fresh)
    image = {}
    for x in range(lx):
        for z in range(lz):
            box = add(state[x, z], neighbours(x, z))
            image[x, z] = 27.0 * state[x, z] - (box + y_pair(box))
    return state, image


def kernel(
    sizes, res_in, dir_in, img_in, gram_in, back_out, small_out,
    res, prev, prev_img, gram, small, land, strip, halo, done, back, part, parts,
    local_sem, send_a, send_b, send_c, recv_sem,
):
    ngx, ngy, ngz, n, lx, lz, width = sizes
    s = lx * lz
    gx, gy, gz = lax.axis_index("gx"), lax.axis_index("gy"), lax.axis_index("gz")
    column = gx * ngz + gz
    place = gy * n + column
    everyone = n * ngy

    loads = [
        pltpu.make_async_copy(a, b, local_sem.at[i])
        for i, (a, b) in enumerate(((res_in, res), (gram_in, gram), (dir_in, prev), (img_in, prev_img)))
    ]
    for load in loads:
        load.start()

    ways = sorted(
        ((dx, dy, dz) for dx in range(ngx) for dy in range(ngy) for dz in range(ngz)),
        key=lambda way: (-min(way[2], ngz - way[2]), -min(way[0], ngx - way[0]), -way[1]),
    )[:-1]

    def peer(offset):
        dx, dy, dz = ways[offset - 1]
        ox, oy, oz = lax.rem(gx + dx, ngx), lax.rem(gy + dy, ngy), lax.rem(gz + dz, ngz)
        return ox * ngz + oz, {"gx": ox, "gy": oy, "gz": oz}

    barrier = pltpu.get_barrier_semaphore()
    for offset in range(1, everyone):
        pl.semaphore_signal(barrier, inc=1, device_id=peer(offset)[1], device_id_type=MESH)
    loads[0].wait()
    depth = width // s
    lanes = lax.broadcasted_iota(jnp.int32, (n, width), 1)
    packed = jnp.zeros((n, width), jnp.float32)
    for i in range(s):
        line = res[pl.ds(i, n, stride=s), :]
        line = pltpu.roll(line, lax.rem(i * depth + jnp.where(gy == 0, depth, 0), width), 1)
        packed = jnp.where(lanes // depth == i, line, packed)
    for i in range(n):
        strip[i] = packed[i : i + 1, :]
    pl.semaphore_wait(barrier, everyone - 1)

    sent = []
    mine = land.at[pl.ds(column * s, s), :]
    for offset in range(1, everyone):
        oc, where = peer(offset)
        near = ways[offset - 1][1] == 0
        copy = pltpu.make_async_remote_copy(
            src_ref=res.at[pl.ds(oc * s, s), :] if near else strip.at[oc],
            dst_ref=mine if near else halo.at[column],
            send_sem=send_a.at[offset], recv_sem=recv_sem.at[0 if near else 3],
            device_id=where, device_id_type=MESH,
        )
        copy.start()
        sent.append(copy)
    pltpu.make_async_copy(res.at[pl.ds(column * s, s), :], mine, recv_sem.at[0]).start()

    def flat(ref, first, stride):
        return jnp.concatenate([ref[pl.ds(first + i, n, stride=stride), :] for i in range(s)], axis=1)

    for load in loads[1:4]:
        load.wait()
    eye = (lax.broadcasted_iota(jnp.int32, (n, n), 0) == lax.broadcasted_iota(jnp.int32, (n, n), 1)).astype(jnp.float32)
    inverse = eliminate(gram[...], eye)
    p, q, r = flat(prev, 0, s), flat(prev_img, 0, s), flat(res, 0, s)
    gram_pq = dot_nt(p, q)

    pltpu.make_async_copy(land, land, recv_sem.at[0]).wait()
    pltpu.make_async_copy(halo, halo, recv_sem.at[3]).wait()
    rows = jnp.concatenate([halo[i] for i in range(n)], axis=0)
    outside = jnp.where(gy == 0, 0, s - 1)

    def extended(i):
        shift = lax.rem((2 * s - i + outside) * depth, width)
        beside = jnp.where(lanes // depth == outside, pltpu.roll(rows, shift, 1), 0.0)
        return jnp.concatenate([land[pl.ds(i, n, stride=s), :], beside], axis=1)

    field = [[extended(x * lz + z) for z in range(lz)] for x in range(lx)]
    state, image = smooth(field, ngx, ngz, gy, width)
    for x in range(lx):
        for z in range(lz):
            first = x * lz + z
            done[pl.ds(first, n, stride=2 * s), :] = state[x, z][:, :width]
            done[pl.ds(first + s, n, stride=2 * s), :] = image[x, z][:, :width]
    mine = back.at[pl.ds(column * 2 * s, 2 * s), :]
    for offset, (dx, _, dz) in enumerate(way for way in ways if way[1] == 0):
        oc = lax.rem(gx + dx, ngx) * ngz + lax.rem(gz + dz, ngz)
        copy = pltpu.make_async_remote_copy(
            src_ref=done.at[pl.ds(oc * 2 * s, 2 * s), :], dst_ref=mine,
            send_sem=send_b.at[offset], recv_sem=recv_sem.at[1],
            device_id={"gx": oc // ngz, "gy": gy, "gz": lax.rem(oc, ngz)}, device_id_type=MESH,
        )
        copy.start()
        sent.append(copy)
    pltpu.make_async_copy(done.at[pl.ds(column * 2 * s, 2 * s), :], mine, recv_sem.at[1]).start()
    pltpu.make_async_copy(back, back, recv_sem.at[1]).wait()

    zf, wf = flat(back, 0, 2 * s), flat(back, s, 2 * s)
    sums = dot_nt(zf, jnp.concatenate([r, wf, q], axis=0))
    sums = jnp.concatenate([sums, gram_pq], axis=1)
    keep = pltpu.make_async_copy(back, back_out, local_sem.at[0])
    keep.start()
    half = n // 2
    part[...] = jnp.concatenate([sums[:half], sums[half:]], axis=1)
    mine = parts.at[pl.ds(place * half, half), :]
    for offset in range(1, everyone):
        copy = pltpu.make_async_remote_copy(
            src_ref=part, dst_ref=mine,
            send_sem=send_c.at[offset], recv_sem=recv_sem.at[2], device_id=peer(offset)[1], device_id_type=MESH,
        )
        copy.start()
        sent.append(copy)
    pltpu.make_async_copy(part, mine, recv_sem.at[2]).start()
    pltpu.make_async_copy(parts, parts, recv_sem.at[2]).wait()

    level = [parts[i * half : (i + 1) * half, :] for i in range(everyone)]
    while len(level) > 1:
        level = [sum(level[i + 1 : i + 2], level[i]) for i in range(0, len(level), 2)]
    total = level[0]
    small[:half, :] = total
    small[half:, :] = jnp.concatenate([inverse[:half], inverse[half:], jnp.zeros((half, 6 * n), jnp.float32)], axis=1)
    store = pltpu.make_async_copy(small, small_out, local_sem.at[1])
    store.start()
    for copy in sent:
        copy.wait_send()
    keep.wait()
    store.wait()


def finish(
    sizes, sol_in, res_in, dir_in, img_in, back_in, small_in, sol_out, res_out, dir_out,
    sol, res, prev, prev_img, back, small, outs, local_sem,
):
    ngx, ngy, ngz, n, lx, lz, width = sizes
    s, half = lx * lz, n // 2
    loads = [
        pltpu.make_async_copy(a, b, local_sem.at[i])
        for i, (a, b) in enumerate(
            ((small_in, small), (dir_in, prev), (img_in, prev_img), (back_in, back), (sol_in, sol), (res_in, res))
        )
    ]
    for load in loads:
        load.start()

    def flat(ref, first, stride):
        return jnp.concatenate([ref[pl.ds(first + i, n, stride=stride), :] for i in range(s)], axis=1)

    loads[0].wait()
    total = small[:half, :]
    inverse = small[half:, :]
    inverse = jnp.concatenate([inverse[:, :n], inverse[:, n : 2 * n]], axis=0)
    total = jnp.concatenate([total[:, : 4 * n], total[:, 4 * n :]], axis=0)
    gram_zr, gram_zw, gram_zq, gram_pq = (total[:, i * n : (i + 1) * n] for i in range(4))

    beta = dot(inverse, gram_zr)
    cross = dot(jnp.concatenate([gram_zq, gram_pq], axis=0), beta)
    beta_t = beta.T
    curvature = gram_zw + cross[:n] + cross[:n].T + dot(beta_t, cross[n:])
    for load in loads[1:4]:
        load.wait()
    p, q, zf, wf = flat(prev, 0, s), flat(prev_img, 0, s), flat(back, 0, 2 * s), flat(back, s, 2 * s)
    mixed = dot(beta_t, jnp.concatenate([p, q], axis=1))
    direction = zf + mixed[:, : s * width]
    image_new = wf + mixed[:, s * width :]
    alpha = eliminate(curvature, gram_zr)
    step = dot(alpha.T, jnp.concatenate([direction, image_new], axis=1))
    loads[4].wait()
    loads[5].wait()
    for i in range(s):
        rows = pl.ds(i, n, stride=s)
        cut = slice(i * width, (i + 1) * width)
        outs[2, rows, :] = direction[:, cut]
        outs[0, rows, :] = sol[rows, :] + step[:, cut]
        outs[1, rows, :] = res[rows, :] - step[:, s * width + i * width : s * width + (i + 1) * width]
    stores = [
        pltpu.make_async_copy(outs.at[i], out, local_sem.at[i]) for i, out in enumerate((sol_out, res_out, dir_out))
    ]
    for store in stores:
        store.start()
    for store in stores:
        store.wait()


def whole_body(sizes, solution, residual, direction_prev, image_prev, gram_prev):
    ngx, ngy, ngz, n, lx, lz, width = sizes
    s, everyone = lx * lz, n * ngy
    rows = n * s
    shape = residual.shape
    field = jax.ShapeDtypeStruct((rows, width), jnp.float32)
    anywhere = pl.BlockSpec(memory_space=pl.ANY)
    block = pltpu.VMEM((rows, width), jnp.float32)
    packed = pltpu.VMEM((n, 8 * n), jnp.float32)
    solution, residual, direction_prev, image_prev = (
        a.reshape(rows, width) for a in (solution, residual, direction_prev, image_prev)
    )
    back, small = pl.pallas_call(
        functools.partial(kernel, sizes),
        out_shape=(
            jax.ShapeDtypeStruct((2 * rows, width), jnp.float32),
            jax.ShapeDtypeStruct((n, 8 * n), jnp.float32),
        ),
        in_specs=[anywhere] * 4,
        out_specs=[anywhere] * 2,
        scratch_shapes=[
            block, block, block,
            pltpu.VMEM((n, n), jnp.float32),
            packed,
            pltpu.VMEM((rows, width), jnp.float32),
            pltpu.VMEM((n, 1, width), jnp.float32),
            pltpu.VMEM((n, 1, width), jnp.float32),
            pltpu.VMEM((2 * rows, width), jnp.float32),
            pltpu.VMEM((2 * rows, width), jnp.float32),
            pltpu.VMEM((n // 2, 8 * n), jnp.float32),
            pltpu.VMEM((everyone * (n // 2), 8 * n), jnp.float32),
            pltpu.SemaphoreType.DMA((4,)),
            pltpu.SemaphoreType.DMA((everyone,)),
            pltpu.SemaphoreType.DMA((n,)),
            pltpu.SemaphoreType.DMA((everyone,)),
            pltpu.SemaphoreType.DMA((4,)),
        ],
        compiler_params=pltpu.CompilerParams(collective_id=0, has_side_effects=True),
    )(residual, direction_prev, image_prev, gram_prev)
    outs = pl.pallas_call(
        functools.partial(finish, sizes),
        out_shape=(field, field, field),
        in_specs=[anywhere] * 6,
        out_specs=[anywhere] * 3,
        scratch_shapes=[
            block, block, block, block,
            pltpu.VMEM((2 * rows, width), jnp.float32),
            packed,
            pltpu.VMEM((3, rows, width), jnp.float32),
            pltpu.SemaphoreType.DMA((6,)),
        ],
    )(solution, residual, direction_prev, image_prev, back, small)
    return tuple(a.reshape(shape) for a in outs)


def pick_body(mesh, solution, residual, direction_prev, image_prev, gram_prev):
    ngx, ngy, ngz = (mesh.shape[axis] for axis in ("gx", "gy", "gz"))
    n, lx, lz, width = residual.shape
    fits = n == ngx * ngz and lx % 2 == 0 and lz % 2 == 0 and (lx * lz) % 8 == 0
    fits = fits and width % 128 == 0 and n % 16 == 0 and ngy == 2 and width % (lx * lz) == 0 and width // (lx * lz) >= 15
    args = (solution, residual, direction_prev, image_prev, gram_prev)
    if fits:
        return whole_body((ngx, ngy, ngz, n, lx, lz, width), *args)
    return body(*args)


def solution(mesh):
    in_specs = (
        P(None, "gx", "gz", "gy"),
        P(None, "gx", "gz", "gy"),
        P(None, "gx", "gz", "gy"),
        P(None, "gx", "gz", "gy"),
        P(),
    )
    out_specs = (P(None, "gx", "gz", "gy"), P(None, "gx", "gz", "gy"), P(None, "gx", "gz", "gy"))
    return jax.shard_map(functools.partial(pick_body, mesh), mesh=mesh, in_specs=in_specs, out_specs=out_specs, check_vma=False)
```

profile of v0, /device:TPU:0, one launch (start us, length us, event | category | flops | bytes accessed | tf_op | source)
XLA Modules:
  0.0 28.6 jit_solution(16139167945774520036)
XLA Ops:
  0.6 24.0 %shard_map.76 = (f32[256,128]{1,0:T(8,128)}, f32[16,128]{1,0:T(8,128)}) custom-call(f32[128,128]{1,0:T(8,128)} %bitcast.7, f32[128,128]{1,0:T(8,128)} %bitcast.9, f32[128,128]{1,0:T(8,128)} %bitcast.11, f32[16,16]{1,0:T(8,128)} %gram_in.1), custom_call_target="tpu_custom_call" | custom-call | tf_op jit(solution)/shard_map/pallas_call | solution.py:406
  24.7 3.9 %shard_map.77 = (f32[128,128]{1,0:T(8,128)}, f32[128,128]{1,0:T(8,128)}, f32[128,128]{1,0:T(8,128)}) custom-call(f32[128,128]{1,0:T(8,128)} %bitcast.13, f32[128,128]{1,0:T(8,128)} %bitcast.8, f32[128,128]{1,0:T(8,128)} %bitcast.10, f32[128,128]{1,0:T(8,128)} %bitcast.12, f32[256,128]{1,0:T(8,128)} %get-tuple-element.8.back_in, ...), custom_call_target="tpu_custom_call" | custom-call | tf_op jit(solution)/shard_map/pallas_call | solution.py:433
where the time goes:
time: 28.8 us; the launch traced here: 28.6 us
  Pallas kernels  27.9 us (97%)
  between operations  0.64 us (2%)
    pallas_call x1, Pallas kernels, whole_body(): pl.pallas_call(functools.partial(kernel, sizes), out_shape=(jax.ShapeDtyp...  24 us
    pallas_call x1, Pallas kernels, whole_body(): pl.pallas_call(functools.partial(finish, sizes), out_shape=(field, field,...  3.92 us

commit v1 on v0

v1 whole, which is shorter than its diff:
```python
import functools

import jax
import jax.numpy as jnp
from jax import lax
from jax.experimental import pallas as pl
from jax.experimental.pallas import tpu as pltpu
from jax.sharding import PartitionSpec as P


def with_halo(value, sides, width):
    for axis, dim in sides:
        devices, length = (lax.axis_size(axis), value.shape[dim])
        up = [(i, (i + 1) % devices) for i in range(devices - 1)]
        down = [(j, i) for i, j in up]
        last = lax.slice_in_dim(value, length - width, length, axis=dim)
        first = lax.slice_in_dim(value, 0, width, axis=dim)
        before = lax.ppermute(last, axis, up)
        after = lax.ppermute(first, axis, down)
        value = jnp.concatenate([before, value, after], axis=dim)
    return value


def box_sum(padded):
    total = padded[:, :-2] + padded[:, 1:-1] + padded[:, 2:]
    total = total[:, :, :-2] + total[:, :, 1:-1] + total[:, :, 2:]
    return total[:, :, :, :-2] + total[:, :, :, 1:-1] + total[:, :, :, 2:]


def colors_of(shape):
    first = lax.broadcasted_iota(jnp.int32, shape, 1) % 2
    second = lax.broadcasted_iota(jnp.int32, shape, 2) % 2
    third = lax.broadcasted_iota(jnp.int32, shape, 3) % 2
    return 4 * first + 2 * second + third


def local_gram(left, right):
    return jnp.einsum("kxzy,lxzy->kl", left, right, precision=lax.Precision.HIGHEST)


def combine(field, mixing):
    return jnp.einsum("kxzy,kl->lxzy", field, mixing, precision=lax.Precision.HIGHEST)


def small_dot(left, right):
    return jnp.dot(left, right, precision=lax.Precision.HIGHEST)


def spd_solve(matrix, target):
    order = matrix.shape[0]
    sym = 0.5 * (matrix + matrix.T)
    lower = jnp.zeros_like(sym)
    for col in range(order):
        column = sym[col:, col] - jnp.sum(lower[col:, :col] * lower[col, :col][None, :], axis=1)
        pivot = jnp.sqrt(column[0])
        lower = lower.at[col:, col].set(column / pivot)
    middle = jnp.zeros_like(target)
    for row in range(order):
        value = target[row] - jnp.sum(lower[row, :row][:, None] * middle[:row], axis=0)
        middle = middle.at[row].set(value / lower[row, row])
    answer = jnp.zeros_like(target)
    for row in range(order - 1, -1, -1):
        value = middle[row] - jnp.sum(lower[row + 1 :, row][:, None] * answer[row + 1 :], axis=0)
        answer = answer.at[row].set(value / lower[row, row])
    return answer


def sweep_box(field):
    padded = with_halo(field, (("gx", 1), ("gy", 3), ("gz", 2)), 1)
    return box_sum(padded)


def body(solution, residual, direction_prev, image_prev, gram_prev):
    colors = colors_of(residual.shape)
    smoothed = jnp.where(colors == 0, residual / 26.0, jnp.float32(0.0))
    for shade in list(range(1, 8)) + list(range(6, -1, -1)):
        boxed = sweep_box(smoothed)
        smoothed = jnp.where(colors == shade, (residual + boxed - smoothed) / 26.0, smoothed)
    padded = with_halo(smoothed, (("gx", 1), ("gy", 3), ("gz", 2)), 1)
    image = 27.0 * smoothed - box_sum(padded)
    sums = (
        local_gram(smoothed, residual),
        local_gram(smoothed, image),
        local_gram(smoothed, image_prev),
        local_gram(direction_prev, image),
        local_gram(direction_prev, image_prev),
    )
    gram_zr, gram_zw, gram_zq, gram_pw, gram_pq = lax.psum(
        (sums[0], sums[1], sums[2], sums[3], sums[4]), ("gx", "gy", "gz")
    )
    beta_mix = spd_solve(gram_prev, gram_zr)
    direction = smoothed + combine(direction_prev, beta_mix)
    image_new = image + combine(image_prev, beta_mix)
    curvature = gram_zw + small_dot(gram_zq, beta_mix) + small_dot(beta_mix.T, gram_pw)
    curvature = curvature + small_dot(small_dot(beta_mix.T, gram_pq), beta_mix)
    alpha_step = spd_solve(curvature, gram_zr)
    solution_new = solution + combine(direction, alpha_step)
    residual_new = residual - combine(image_new, alpha_step)
    return (solution_new, residual_new, direction)


MESH = pl.DeviceIdType.MESH
HIGHEST = lax.Precision.HIGHEST


def dot(left, right):
    return jnp.dot(left, right, precision=HIGHEST, preferred_element_type=jnp.float32)


def dot_nt(left, right):
    return lax.dot_general(
        left, right, (((1,), (1,)), ((), ())), precision=HIGHEST, preferred_element_type=jnp.float32
    )


def eliminate(matrix, target):
    order = matrix.shape[0]
    rows = lax.broadcasted_iota(jnp.int32, matrix.shape, 0)
    columns = [jnp.broadcast_to(matrix[:, k : k + 1], matrix.shape) for k in range(order)]
    scale = jnp.zeros(matrix.shape, jnp.float32)
    for c in range(order):
        inverse = 1.0 / columns[c][c : c + 1, :]
        here = rows == c
        factor = jnp.where(here, 0.0, columns[c] * inverse)
        for k in range(c + 1, order):
            columns[k] = columns[k] - factor * columns[k][c : c + 1, :]
        target = target - factor * target[c : c + 1, :]
        scale = jnp.where(here, inverse, scale)
    return target * scale


def smooth(res, ngx, ngz, gy, width, emit):
    lx, lz = len(res), len(res[0])
    count, ny = res[0][0].shape
    row = lax.broadcasted_iota(jnp.int32, (count, ny), 0)
    lane = lax.broadcasted_iota(jnp.int32, (count, ny), 1)
    even = lane % 2 == 0
    edges = {
        "xp": (row < ngz, ngz, 0),
        "xn": (row >= count - ngz, count - ngz, 0),
        "zp": (row % ngz == 0, 1, 0),
        "zn": (row % ngz == ngz - 1, count - 1, 0),
        "yp": (lane == jnp.where(gy == 0, 0, -1), 1, 1),
        "yn": (lane == jnp.where(gy == 0, -1, width - 1), ny - 1, 1),
    }
    zero = jnp.zeros((count, ny), jnp.float32)
    memo = {}

    def moved(value, kind):
        if value is None:
            return None
        key = (kind, id(value))
        if key not in memo:
            edge, amount, axis = edges[kind]
            memo[key] = (value, jnp.where(edge, zero, pltpu.roll(value, amount, axis)))
        return memo[key][1]

    def add(*values):
        total = None
        for value in values:
            if value is not None:
                total = value if total is None else total + value
        return total

    state = {(x, z): None for x in range(lx) for z in range(lz)}

    def z_pair(x, z):
        before = state[x, z - 1] if z > 0 else moved(state[x, lz - 1], "zp")
        after = state[x, z + 1] if z < lz - 1 else moved(state[x, 0], "zn")
        return add(before, after)

    def neighbours(x, z):
        def line(other):
            return add(state[other, z], z_pair(other, z))

        before = line(x - 1) if x > 0 else moved_line(lx - 1, z, "xp")
        after = line(x + 1) if x < lx - 1 else moved_line(0, z, "xn")
        return add(z_pair(x, z), before, after)

    def moved_line(x, z, kind):
        return moved(add(state[x, z], z_pair(x, z)), kind)

    def y_pair(value):
        return moved(value, "yp") + moved(value, "yn")

    third = jnp.float32(1.0 / 26.0)
    plan = [(0, 0, (0, 1)), (0, 1, (0, 1)), (1, 0, (0, 1)), (1, 1, (0, 1, 0)), (1, 0, (1, 0)), (0, 1, (1, 0)), (0, 0, (1, 0))]
    forward = {}
    for step, (xp, zp, shades) in enumerate(plan):
        fresh = {}
        for x in range(xp, lx, 2):
            for z in range(zp, lz, 2):
                near = neighbours(x, z)
                base = res[x][z] if near is None else res[x][z] + (near + y_pair(near))
                value = state[x, z]
                for turn, shade in enumerate(shades):
                    total = base if value is None else base + y_pair(value)
                    chosen = even if shade == 0 else jnp.logical_not(even)
                    value = jnp.where(chosen, total * third, zero if value is None else value)
                    if turn == 1 and step < 4:
                        forward[x, z] = value
                fresh[x, z] = value
        state.update(fresh)
        emit(step, forward, state)
    image = {}
    for x in range(lx):
        for z in range(lz):
            box = add(state[x, z], neighbours(x, z))
            image[x, z] = 27.0 * state[x, z] - (box + y_pair(box))
    return image


def pack(value):
    rows = value.shape[0] * value.shape[1] // 128
    return jnp.concatenate([value[i : i + rows] for i in range(0, value.shape[0], rows)], axis=1)


def unpack(value, lanes):
    return jnp.concatenate([value[:, i : i + lanes] for i in range(0, value.shape[1], lanes)], axis=0)


def tree_sum(values):
    while len(values) > 1:
        values = [sum(values[i + 1 : i + 2], values[i]) for i in range(0, len(values), 2)]
    return values[0]


def kernel(
    sizes, sol_in, res_in, dir_in, img_in, gram_in, sol_out, res_out, dir_out,
    sol, res, prev, prev_img, gram, land, strip, halo, done, back, part, parts,
    local_sem, send_sem, recv_sem,
):
    ngx, ngy, ngz, n, lx, lz, width = sizes
    s = lx * lz
    half, stretch = s // 2, 5 * s
    gx, gy, gz = lax.axis_index("gx"), lax.axis_index("gy"), lax.axis_index("gz")
    column = gx * ngz + gz
    place = gy * n + column
    everyone = n * ngy

    loads = [
        pltpu.make_async_copy(a, b, local_sem.at[i])
        for i, (a, b) in enumerate(
            ((res_in, res), (gram_in, gram), (dir_in, prev), (img_in, prev_img), (sol_in, sol))
        )
    ]
    for load in loads:
        load.start()

    ways = sorted(
        ((dx, dy, dz) for dx in range(ngx) for dy in range(ngy) for dz in range(ngz)),
        key=lambda way: (-min(way[2], ngz - way[2]), -min(way[0], ngx - way[0]), -way[1]),
    )[:-1]
    flock = []
    for dx, dy, dz in ways:
        ox, oy, oz = lax.rem(gx + dx, ngx), lax.rem(gy + dy, ngy), lax.rem(gz + dz, ngz)
        flock.append((dy == 0, ox * ngz + oz, {"gx": ox, "gy": oy, "gz": oz}))

    def remote(source, target, sent, arrived, where):
        pltpu.make_async_remote_copy(
            src_ref=source, dst_ref=target, send_sem=send_sem.at[sent], recv_sem=recv_sem.at[arrived],
            device_id=where, device_id_type=MESH,
        ).start()

    def wait(ref, semaphore):
        pltpu.make_async_copy(ref, ref, semaphore).wait()

    barrier = pltpu.get_barrier_semaphore()
    for _, _, where in flock:
        pl.semaphore_signal(barrier, inc=1, device_id=where, device_id_type=MESH)
    loads[0].wait()
    depth = width // s
    lanes = lax.broadcasted_iota(jnp.int32, (n, width), 1)
    packed = jnp.zeros((n, width), jnp.float32)
    for i in range(s):
        line = res[pl.ds(i, n, stride=s), :]
        line = pltpu.roll(line, lax.rem(i * depth + jnp.where(gy == 0, depth, 0), width), 1)
        packed = jnp.where(lanes // depth == i, line, packed)
    for i in range(n):
        strip[i] = packed[i : i + 1, :]
    pl.semaphore_wait(barrier, everyone - 1)

    mine = land.at[pl.ds(column * s, s), :]
    for near, oc, where in flock:
        if near:
            remote(res.at[pl.ds(oc * s, s), :], mine, 0, 0, where)
        else:
            remote(strip.at[oc], halo.at[column], 0, 1, where)
    pltpu.make_async_copy(res.at[pl.ds(column * s, s), :], mine, recv_sem.at[0]).start()

    def flat(ref, offsets, stride):
        return jnp.concatenate([ref[pl.ds(i, n, stride=stride), :] for i in offsets], axis=1)

    def place_of(x, z, final):
        slot = x % 2 if final == 0 else 3 - x % 2
        return slot * s + x // 2 * lz + z

    planes = [(x, z) for x in range(lx) for z in range(lz)]
    for load in loads[1:4]:
        load.wait()
    eye = (lax.broadcasted_iota(jnp.int32, (n, n), 0) == lax.broadcasted_iota(jnp.int32, (n, n), 1)).astype(jnp.float32)
    inverse = eliminate(0.5 * (gram[...] + gram[...].T), eye)
    p, q = flat(prev, range(s), s), flat(prev_img, range(s), s)
    gram_pq = dot_nt(p, q)

    wait(land, recv_sem.at[0])
    wait(halo, recv_sem.at[1])
    rows = jnp.concatenate([halo[i] for i in range(n)], axis=0)
    outside = jnp.where(gy == 0, 0, s - 1)

    def extended(i):
        shift = lax.rem((2 * s - i + outside) * depth, width)
        beside = jnp.where(lanes // depth == outside, pltpu.roll(rows, shift, 1), 0.0)
        return jnp.concatenate([land[pl.ds(i, n, stride=s), :], beside], axis=1)

    def give(first, count, arrived):
        target = back.at[pl.ds(column * stretch + first, count), :]
        for near, oc, where in flock:
            if near:
                remote(done.at[pl.ds(oc * stretch + first, count), :], target, 1, arrived, where)
        pltpu.make_async_copy(
            done.at[pl.ds(column * stretch + first, count), :], target, recv_sem.at[arrived]
        ).start()

    def emit(step, forward, state):
        if step not in (1, 3, 4, 6):
            return
        final = 0 if step < 4 else 1
        odd = 1 if step in (3, 4) else 0
        values = state if final else forward
        for x, z in planes:
            if x % 2 == odd:
                done[pl.ds(place_of(x, z, final), n, stride=stretch), :] = values[x, z][:, :width]
        give(place_of(odd, 0, final), half, 2 + final)

    field = [[extended(x * lz + z) for z in range(lz)] for x in range(lx)]
    image = smooth(field, ngx, ngz, gy, width, emit)
    for i, (x, z) in enumerate(planes):
        done[pl.ds(4 * s + i, n, stride=stretch), :] = image[x, z][:, :width]
    give(4 * s, s, 4)

    def share(index, sums):
        part[index] = pack(sums)
        for _, _, where in flock:
            remote(part.at[index], parts.at[index, place], 2 + index, 5 + index, where)
        pltpu.make_async_copy(part.at[index], parts.at[index, place], recv_sem.at[5 + index]).start()

    def shared(index):
        wait(parts.at[index], recv_sem.at[5 + index])
        total = unpack(tree_sum([parts[index, i] for i in range(everyone)]), 2 * n)
        return total[:, :n], total[:, n:]

    wait(back.at[pl.ds(0, n * s), :], recv_sem.at[2])
    yf = flat(back, [place_of(x, z, 0) for x, z in planes], stretch)
    share(0, jnp.concatenate([26.0 * dot_nt(yf, yf), gram_pq], axis=1))

    wait(back.at[pl.ds(0, n * s), :], recv_sem.at[3])
    zf = flat(back, [place_of(x, z, 1) for x, z in planes], stretch)
    uf = zf - yf
    share(1, jnp.concatenate([dot_nt(uf, uf), dot_nt(zf, q)], axis=1))

    gram_zr, gram_pq = shared(0)
    beta = dot(inverse, gram_zr)
    beta_t = beta.T
    known = gram_zr + dot(beta_t, dot(gram_pq, beta))
    mixed = dot(beta_t, jnp.concatenate([p, q], axis=1))
    direction = zf + mixed[:, : s * width]
    wait(back.at[pl.ds(0, n * s), :], recv_sem.at[4])
    wf = flat(back, [4 * s + i for i in range(s)], stretch)
    both = jnp.concatenate([direction, wf + mixed[:, s * width :]], axis=1)
    for i in range(s):
        dir_out[pl.ds(i, n, stride=s), :] = direction[:, i * width : (i + 1) * width]
    loads[4].wait()
    wait(done.at[pl.ds(0, (n - 1) * s + n), :], send_sem.at[0])
    wait(done.at[pl.ds(0, (n - 1) * 3 * s), :], send_sem.at[1])
    wait(parts.at[0, pl.ds(0, everyone - 1)], send_sem.at[2])

    gram_uu, gram_zq = shared(1)
    curvature = known - 26.0 * gram_uu + dot(gram_zq, beta) + dot_nt(beta_t, gram_zq)
    alpha = eliminate(curvature, gram_zr)
    step = dot(alpha.T, both)
    for i in range(s):
        rows = pl.ds(i, n, stride=s)
        sol_out[rows, :] = sol[rows, :] + step[:, i * width : (i + 1) * width]
        res_out[rows, :] = res[rows, :] - step[:, (s + i) * width : (s + i + 1) * width]
    wait(parts.at[1, pl.ds(0, everyone - 1)], send_sem.at[3])


def write(*refs):
    half = len(refs) // 2
    semaphore = refs[-1]
    stores = [pltpu.make_async_copy(refs[i], refs[half + i], semaphore.at[i]) for i in range(half)]
    for store in stores:
        store.start()
    for store in stores:
        store.wait()


def whole_body(sizes, *args):
    ngx, ngy, ngz, n, lx, lz, width = sizes
    s, everyone = lx * lz, n * ngy
    rows = n * s
    shape = args[0].shape
    field = jax.ShapeDtypeStruct((rows, width), jnp.float32)
    anywhere = pl.BlockSpec(memory_space=pl.ANY)
    inside = pl.BlockSpec(memory_space=pltpu.VMEM)
    block = pltpu.VMEM((rows, width), jnp.float32)
    packed = 2 * n * n // 128
    outs = pl.pallas_call(
        functools.partial(kernel, sizes),
        out_shape=(block,) * 3,
        in_specs=[anywhere] * 5,
        out_specs=[inside] * 3,
        scratch_shapes=[
            block, block, block, block,
            pltpu.VMEM((n, n), jnp.float32),
            block,
            pltpu.VMEM((n, 1, width), jnp.float32),
            pltpu.VMEM((n, 1, width), jnp.float32),
            pltpu.VMEM((5 * rows, width), jnp.float32),
            pltpu.VMEM((5 * rows, width), jnp.float32),
            pltpu.VMEM((2, packed, 128), jnp.float32),
            pltpu.VMEM((2, everyone, packed, 128), jnp.float32),
            pltpu.SemaphoreType.DMA((5,)),
            pltpu.SemaphoreType.DMA((4,)),
            pltpu.SemaphoreType.DMA((7,)),
        ],
        compiler_params=pltpu.CompilerParams(
            collective_id=0, has_side_effects=True
        ),
    )(*(a.reshape(rows, width) for a in args[:4]), args[4])
    outs = [pltpu.with_memory_space_constraint(a, pltpu.VMEM) for a in outs]
    outs = pl.pallas_call(
        write,
        out_shape=(field,) * 3,
        in_specs=[inside] * 3,
        out_specs=[anywhere] * 3,
        scratch_shapes=[pltpu.SemaphoreType.DMA((3,))],

    )(*outs)
    return tuple(a.reshape(shape) for a in outs)


def pick_body(mesh, solution, residual, direction_prev, image_prev, gram_prev):
    ngx, ngy, ngz = (mesh.shape[axis] for axis in ("gx", "gy", "gz"))
    n, lx, lz, width = residual.shape
    fits = n == ngx * ngz and lx % 2 == 0 and lz % 2 == 0 and (lx * lz) % 8 == 0
    fits = fits and width % 128 == 0 and n % 16 == 0 and 128 % (2 * n) == 0 and ngy == 2 and width % (lx * lz) == 0 and width // (lx * lz) >= 15
    args = (solution, residual, direction_prev, image_prev, gram_prev)
    if fits:
        return whole_body((ngx, ngy, ngz, n, lx, lz, width), *args)
    return body(*args)


def solution(mesh):
    in_specs = (
        P(None, "gx", "gz", "gy"),
        P(None, "gx", "gz", "gy"),
        P(None, "gx", "gz", "gy"),
        P(None, "gx", "gz", "gy"),
        P(),
    )
    out_specs = (P(None, "gx", "gz", "gy"), P(None, "gx", "gz", "gy"), P(None, "gx", "gz", "gy"))
    return jax.shard_map(functools.partial(pick_body, mesh), mesh=mesh, in_specs=in_specs, out_specs=out_specs, check_vma=False)
```

time: 28.8 us -> 24.9 us (0.86)
  Pallas kernels: 27.9 us -> 24.1 us
    pallas_call x2, Pallas kernels: 27.9 us -> 24.1 us  [the longest x1 23.4 us: whole_body(): pl.pallas_call(functools.partial(kernel, sizes), out_shape=(block,) * 3,...]
where the time goes in v1:
time: 24.9 us; the launch traced here: 24.7 us
  Pallas kernels  24.1 us (97%)
  between operations  0.64 us (3%)
    pallas_call x1, Pallas kernels, whole_body(): pl.pallas_call(functools.partial(kernel, sizes), out_shape=(block,) * 3,...  23.4 us
    pallas_call x1, Pallas kernels, whole_body(): pl.pallas_call(write, out_shape=(field,) * 3, in_specs=[inside] * 3, out_...  0.7 us

profile of v1, /device:TPU:0, one launch (start us, length us, event | category | flops | bytes accessed | tf_op | source)
XLA Modules:
  0.0 24.7 jit_solution(9520062624788346854)
XLA Ops:
  0.6 23.4 %shard_map.76 = (f32[128,128]{1,0:T(8,128)S(1)}, f32[128,128]{1,0:T(8,128)S(1)}, f32[128,128]{1,0:T(8,128)S(1)}) custom-call(f32[128,128]{1,0:T(8,128)} %bitcast.7, f32[128,128]{1,0:T(8,128)} %bitcast.8, f32[128,128]{1,0:T(8,128)} %bitcast.9, f32[128,128]{1,0:T(8,128)} %bitcast.10, f32[16,16]{1,0:T(8,128)} %gram_in.1), custom_call_target="tpu_custom_call" | custom-call | tf_op jit(solution)/shard_map/pallas_call | solution.py:409
  24.0 0.7 %shard_map.77 = (f32[128,128]{1,0:T(8,128)}, f32[128,128]{1,0:T(8,128)}, f32[128,128]{1,0:T(8,128)}) custom-call(f32[128,128]{1,0:T(8,128)S(1)} %get-tuple-element.9.refs_0_, f32[128,128]{1,0:T(8,128)S(1)} %get-tuple-element.10.refs_1_, f32[128,128]{1,0:T(8,128)S(1)} %get-tuple-element.11.refs_2_), custom_call_target="tpu_custom_call" | custom-call | tf_op jit(solution)/shard_map/pallas_call | solution.py:433

commit v2 on v1

--- a/solution.py
+++ b/solution.py
@@ -129,20 +129,27 @@
     return target * scale
 
 
-def smooth(res, ngx, ngz, gy, width, emit):
+def smooth(res, ngx, ngz, gy, whole, emit):
     lx, lz = len(res), len(res[0])
     count, ny = res[0][0].shape
     row = lax.broadcasted_iota(jnp.int32, (count, ny), 0)
     lane = lax.broadcasted_iota(jnp.int32, (count, ny), 1)
     even = lane % 2 == 0
+    inner = row % (ngx * ngz)
     edges = {
-        "xp": (row < ngz, ngz, 0),
-        "xn": (row >= count - ngz, count - ngz, 0),
-        "zp": (row % ngz == 0, 1, 0),
-        "zn": (row % ngz == ngz - 1, count - 1, 0),
-        "yp": (lane == jnp.where(gy == 0, 0, -1), 1, 1),
-        "yn": (lane == jnp.where(gy == 0, -1, width - 1), ny - 1, 1),
+        "xp": (inner < ngz, ngz),
+        "xn": (inner >= (ngx - 1) * ngz, count - ngz),
+        "zp": (row % ngz == 0, 1),
+        "zn": (row % ngz == ngz - 1, count - 1),
     }
+    first = jnp.where(jnp.logical_and(row < whole, gy == 0), 0, -8)
+    last = jnp.where(jnp.logical_and(row < whole, gy != 0), ny - 1, -8)
+    cut = jnp.where(row < whole, jnp.where(gy == 0, ny - 3, 0), -8)
+    valid = jnp.logical_or(lane < cut, lane > cut + 2)
+    valid_even, valid_odd = jnp.logical_and(valid, even), jnp.logical_and(valid, jnp.logical_not(even))
+    twice = 2.0 - jnp.where(lane == first, 1.0, 0.0) - jnp.where(lane == last, 1.0, 0.0)
+    below = 3.0 - jnp.where(lane == first + 1, 1.0, 0.0) - jnp.where(lane == last, 1.0, 0.0)
+    above = 3.0 - jnp.where(lane == last - 1, 1.0, 0.0) - jnp.where(lane == first, 1.0, 0.0)
     zero = jnp.zeros((count, ny), jnp.float32)
     memo = {}
 
@@ -151,8 +158,8 @@
             return None
         key = (kind, id(value))
         if key not in memo:
-            edge, amount, axis = edges[kind]
-            memo[key] = (value, jnp.where(edge, zero, pltpu.roll(value, amount, axis)))
+            edge, amount = edges[kind]
+            memo[key] = (value, jnp.where(edge, zero, pltpu.roll(value, amount, 0)))
         return memo[key][1]
 
     def add(*values):
@@ -180,33 +187,54 @@
     def moved_line(x, z, kind):
         return moved(add(state[x, z], z_pair(x, z)), kind)
 
-    def y_pair(value):
-        return moved(value, "yp") + moved(value, "yn")
+    def woven(at_even, at_odd):
+        return jnp.where(valid_even, at_even, jnp.where(valid_odd, at_odd, zero))
+
+    def shifted(value, k):
+        return pltpu.roll(value, k, 1), pltpu.roll(value, ny - k, 1)
+
+    def once(value):
+        return sum(shifted(value, 1))
+
+    def two(value):
+        return sum(shifted(value, 2)) + twice * value
 
     third = jnp.float32(1.0 / 26.0)
-    plan = [(0, 0, (0, 1)), (0, 1, (0, 1)), (1, 0, (0, 1)), (1, 1, (0, 1, 0)), (1, 0, (1, 0)), (0, 1, (1, 0)), (0, 0, (1, 0))]
+    plan = [(0, 0), (0, 1), (1, 0), (1, 1), (1, 0), (0, 1), (0, 0)]
     forward = {}
-    for step, (xp, zp, shades) in enumerate(plan):
+    for step, (xp, zp) in enumerate(plan):
         fresh = {}
         for x in range(xp, lx, 2):
             for z in range(zp, lz, 2):
-                near = neighbours(x, z)
-                base = res[x][z] if near is None else res[x][z] + (near + y_pair(near))
-                value = state[x, z]
-                for turn, shade in enumerate(shades):
-                    total = base if value is None else base + y_pair(value)
-                    chosen = even if shade == 0 else jnp.logical_not(even)
-                    value = jnp.where(chosen, total * third, zero if value is None else value)
-                    if turn == 1 and step < 4:
-                        forward[x, z] = value
-                fresh[x, z] = value
+                near, value = neighbours(x, z), state[x, z]
+                own = res[x][z]
+                both = own if near is None else own + near
+                share = third * both
+                if value is None and near is None:
+                    fresh[x, z] = jnp.where(even, share, third * (own + once(woven(share, zero))))
+                    forward[x, z] = fresh[x, z]
+                elif value is None:
+                    mix = woven(near + share, near)
+                    down, up = shifted(mix, 1)
+                    pair, far = down + up, two(mix)
+                    base = both + pair
+                    later = third * (base + third * far)
+                    fresh[x, z] = forward[x, z] = jnp.where(even, third * base, later)
+                    if step == 3:
+                        deep = sum(shifted(mix, 3)) + below * down + above * up
+                        again = base + third * (once(woven(zero, both)) + far + third * deep)
+                        fresh[x, z] = jnp.where(even, third * again, later)
+                else:
+                    mix = woven(near + value, near + share)
+                    base = both + once(mix)
+                    fresh[x, z] = third * jnp.where(even, base + third * two(mix), base)
         state.update(fresh)
         emit(step, forward, state)
     image = {}
     for x in range(lx):
         for z in range(lz):
             box = add(state[x, z], neighbours(x, z))
-            image[x, z] = 27.0 * state[x, z] - (box + y_pair(box))
+            image[x, z] = 27.0 * state[x, z] - (box + once(jnp.where(valid, box, zero)))
     return image
 
 
@@ -225,14 +253,29 @@
     return values[0]
 
 
+def spans_of(ngz, lx, lz):
+    level, spans = ngz // 2, []
+    for plane in range(ngz):
+        rows = []
+        for x in range(lx):
+            for z in range(lz):
+                below = level * lz - 1 - (plane * lz + z)
+                away, reach = (below, 5) if below >= 0 else (-1 - below, 6)
+                if away <= reach - 2 * (x % 2):
+                    rows.append(x * lz + z)
+        spans.append((rows[0], rows[-1] + 1) if rows else (0, 0))
+    return spans
+
+
 def kernel(
     sizes, sol_in, res_in, dir_in, img_in, gram_in, sol_out, res_out, dir_out,
-    sol, res, prev, prev_img, gram, land, strip, halo, done, back, part, parts,
+    sol, res, prev, prev_img, gram, land, strip, halo, done, back, part, parts, early, earlies,
     local_sem, send_sem, recv_sem,
 ):
     ngx, ngy, ngz, n, lx, lz, width = sizes
-    s = lx * lz
-    half, stretch = s // 2, 5 * s
+    s, level = lx * lz, ngz // 2
+    per = n // (ngx * level)
+    some = per * s
     gx, gy, gz = lax.axis_index("gx"), lax.axis_index("gy"), lax.axis_index("gz")
     column = gx * ngz + gz
     place = gy * n + column
@@ -247,14 +290,27 @@
     for load in loads:
         load.start()
 
+    low = gz < level
+    floors = [
+        jnp.where(
+            low,
+            jnp.where(ngz - 1 - k > gz, ngz - 1 - k, ngz - 2 - k),
+            jnp.where(k < gz, k, k + 1),
+        )
+        for k in range(ngz - 1)
+    ] + [gz]
+    across = [jnp.bitwise_xor(gx, dx) for dx in range(ngx)]
     ways = sorted(
-        ((dx, dy, dz) for dx in range(ngx) for dy in range(ngy) for dz in range(ngz)),
-        key=lambda way: (-min(way[2], ngz - way[2]), -min(way[0], ngx - way[0]), -way[1]),
-    )[:-1]
+        ((dx, dy, k) for dx in range(ngx) for dy in range(ngy) for k in range(ngz)),
+        key=lambda way: (way[2] >= level, way[2] - (way[0] > 1) - way[1], -way[1], -way[0]),
+    )
     flock = []
-    for dx, dy, dz in ways:
-        ox, oy, oz = lax.rem(gx + dx, ngx), lax.rem(gy + dy, ngy), lax.rem(gz + dz, ngz)
-        flock.append((dy == 0, ox * ngz + oz, {"gx": ox, "gy": oy, "gz": oz}))
+    for dx, dy, k in ways:
+        if (dx, dy, k) != (0, 0, ngz - 1):
+            ox, oy, oz = across[dx], 1 - gy if dy else gy, floors[k]
+            owner = ox * level + jnp.bitwise_and(oz, level - 1)
+            flock.append((dy == 0, k >= level, owner, ox * ngz + oz, {"gx": ox, "gy": oy, "gz": oz}))
+    owner = gx * level + jnp.bitwise_and(gz, level - 1)
 
     def remote(source, target, sent, arrived, where):
         pltpu.make_async_remote_copy(
@@ -265,9 +321,10 @@
     def wait(ref, semaphore):
         pltpu.make_async_copy(ref, ref, semaphore).wait()
 
+    land[...] = jnp.zeros_like(land)
     barrier = pltpu.get_barrier_semaphore()
-    for _, _, where in flock:
-        pl.semaphore_signal(barrier, inc=1, device_id=where, device_id_type=MESH)
+    for peer in flock:
+        pl.semaphore_signal(barrier, inc=1, device_id=peer[4], device_id_type=MESH)
     loads[0].wait()
     depth = width // s
     lanes = lax.broadcasted_iota(jnp.int32, (n, width), 1)
@@ -280,102 +337,147 @@
         strip[i] = packed[i : i + 1, :]
     pl.semaphore_wait(barrier, everyone - 1)
 
-    mine = land.at[pl.ds(column * s, s), :]
-    for near, oc, where in flock:
-        if near:
-            remote(res.at[pl.ds(oc * s, s), :], mine, 0, 0, where)
-        else:
-            remote(strip.at[oc], halo.at[column], 0, 1, where)
-    pltpu.make_async_copy(res.at[pl.ds(column * s, s), :], mine, recv_sem.at[0]).start()
-
-    def flat(ref, offsets, stride):
-        return jnp.concatenate([ref[pl.ds(i, n, stride=stride), :] for i in offsets], axis=1)
-
-    def place_of(x, z, final):
-        slot = x % 2 if final == 0 else 3 - x % 2
-        return slot * s + x // 2 * lz + z
+    mine = land.at[pl.ds(column * some, some), :]
+    spans = spans_of(ngz, lx, lz)
+
+    def by_plane(work):
+        for span in sorted(set(spans)):
+            here = functools.reduce(jnp.logical_or, [gz == g for g in range(ngz) if spans[g] == span])
+            pl.when(here)(functools.partial(work, *span))
+
+    def cross(begin, end):
+        for same, level_with, into, _, where in flock:
+            if same and not level_with:
+                remote(
+                    res.reshape(n, s, width).at[pl.ds(into * per, per), pl.ds(begin, end - begin), :],
+                    land.reshape(per * n, s, width).at[pl.ds(column * per, per), pl.ds(begin, end - begin), :],
+                    6, 8, where,
+                )
+
+    def edges(level_with_me):
+        for same, level_with, into, _, where in flock:
+            if not same and level_with == level_with_me:
+                remote(strip.at[pl.ds(into * per, per)], halo.at[pl.ds(column * per, per)], 5, 1, where)
+
+    edges(False)
+    by_plane(cross)
+    edges(True)
+    for same, level_with, into, _, where in flock:
+        if same and level_with:
+            remote(res.at[pl.ds(into * some, some), :], mine, 0, 0, where)
+    pltpu.make_async_copy(res.at[pl.ds(owner * some, some), :], mine, recv_sem.at[0]).start()
+
+    def flat(ref, first, stride):
+        return jnp.concatenate([ref[pl.ds(first + i, n, stride=stride), :] for i in range(s)], axis=1)
+
+    def send_all(source, target, sent, arrived):
+        for peer in flock:
+            remote(source, target, sent, arrived, peer[4])
+        pltpu.make_async_copy(source, target, recv_sem.at[arrived]).start()
 
     planes = [(x, z) for x in range(lx) for z in range(lz)]
     for load in loads[1:4]:
         load.wait()
+    p, q = flat(prev, 0, s), flat(prev_img, 0, s)
+    early[0] = pack(dot_nt(p, q))
     eye = (lax.broadcasted_iota(jnp.int32, (n, n), 0) == lax.broadcasted_iota(jnp.int32, (n, n), 1)).astype(jnp.float32)
     inverse = eliminate(0.5 * (gram[...] + gram[...].T), eye)
-    p, q = flat(prev, range(s), s), flat(prev_img, range(s), s)
-    gram_pq = dot_nt(p, q)
-
-    wait(land, recv_sem.at[0])
+
+    wait(land.at[pl.ds(0, level * ngx * some), :], recv_sem.at[0])
+    above = ngx * per * sum(end - begin for begin, end in spans[level:])
+    below = ngx * per * sum(end - begin for begin, end in spans[:level])
+
+    @pl.when(low)
+    def _():
+        wait(land.at[pl.ds(0, above), :], recv_sem.at[8])
+
+    @pl.when(jnp.logical_not(low))
+    def _():
+        wait(land.at[pl.ds(0, below), :], recv_sem.at[8])
+
     wait(halo, recv_sem.at[1])
-    rows = jnp.concatenate([halo[i] for i in range(n)], axis=0)
-    outside = jnp.where(gy == 0, 0, s - 1)
+    beyond = [jnp.concatenate([halo[i * per + a] for i in range(n)], axis=0) for a in range(per)]
+    zone = width // per
+    outer = jnp.where(gy == 0, zone - depth, 0)
+    shift = jnp.where(gy == 0, zone, depth)
 
     def extended(i):
-        shift = lax.rem((2 * s - i + outside) * depth, width)
-        beside = jnp.where(lanes // depth == outside, pltpu.roll(rows, shift, 1), 0.0)
-        return jnp.concatenate([land[pl.ds(i, n, stride=s), :], beside], axis=1)
-
-    def give(first, count, arrived):
-        target = back.at[pl.ds(column * stretch + first, count), :]
-        for near, oc, where in flock:
-            if near:
-                remote(done.at[pl.ds(oc * stretch + first, count), :], target, 1, arrived, where)
-        pltpu.make_async_copy(
-            done.at[pl.ds(column * stretch + first, count), :], target, recv_sem.at[arrived]
-        ).start()
+        lines = [land[pl.ds(a * s + i, n, stride=some), :] for a in range(per)]
+        edge = None
+        for a in range(per):
+            begin = a * zone
+            inside = pltpu.roll(lines[a], lax.rem(begin + shift + jnp.where(gy == 0, width - depth, 0), width), 1)
+            outside = pltpu.roll(beyond[a], lax.rem(begin + outer + width - i * depth, width), 1)
+            at = lanes - (begin + outer)
+            value = jnp.where(jnp.logical_and(at >= 0, at < depth), outside, inside)
+            edge = value if edge is None else jnp.where(lanes >= begin, value, edge)
+        return jnp.concatenate(lines + [edge], axis=0)
+
+    border = jnp.where(gy == 0, width - depth, 0)
+    at_border = jnp.logical_and(lanes >= border, lanes < border + depth)
+
+    def keep(field, values):
+        for i, (x, z) in enumerate(planes):
+            edge = values[x, z][per * n :]
+            for a in range(per):
+                back_shift = lax.rem(2 * width - a * zone - shift - jnp.where(gy == 0, width - depth, 0), width)
+                value = jnp.where(at_border, pltpu.roll(edge, back_shift, 1), values[x, z][a * n : (a + 1) * n])
+                done[field, pl.ds(a * s + i, n, stride=some), :] = value
+        target = back.at[field, pl.ds(owner * some, some), :]
+        for same, level_with, _, home, where in flock:
+            if same and level_with:
+                remote(done.at[field, pl.ds(home * some, some), :], target, 1, 2 + field, where)
+        pltpu.make_async_copy(done.at[field, pl.ds(column * some, some), :], target, recv_sem.at[2 + field]).start()
 
     def emit(step, forward, state):
-        if step not in (1, 3, 4, 6):
-            return
-        final = 0 if step < 4 else 1
-        odd = 1 if step in (3, 4) else 0
-        values = state if final else forward
-        for x, z in planes:
-            if x % 2 == odd:
-                done[pl.ds(place_of(x, z, final), n, stride=stretch), :] = values[x, z][:, :width]
-        give(place_of(odd, 0, final), half, 2 + final)
+        if step == 3:
+            keep(0, forward)
+        if step == 6:
+            keep(1, state)
 
     field = [[extended(x * lz + z) for z in range(lz)] for x in range(lx)]
-    image = smooth(field, ngx, ngz, gy, width, emit)
-    for i, (x, z) in enumerate(planes):
-        done[pl.ds(4 * s + i, n, stride=stretch), :] = image[x, z][:, :width]
-    give(4 * s, s, 4)
-
-    def share(index, sums):
-        part[index] = pack(sums)
-        for _, _, where in flock:
-            remote(part.at[index], parts.at[index, place], 2 + index, 5 + index, where)
-        pltpu.make_async_copy(part.at[index], parts.at[index, place], recv_sem.at[5 + index]).start()
-
-    def shared(index):
-        wait(parts.at[index], recv_sem.at[5 + index])
-        total = unpack(tree_sum([parts[index, i] for i in range(everyone)]), 2 * n)
-        return total[:, :n], total[:, n:]
-
-    wait(back.at[pl.ds(0, n * s), :], recv_sem.at[2])
-    yf = flat(back, [place_of(x, z, 0) for x, z in planes], stretch)
-    share(0, jnp.concatenate([26.0 * dot_nt(yf, yf), gram_pq], axis=1))
-
-    wait(back.at[pl.ds(0, n * s), :], recv_sem.at[3])
-    zf = flat(back, [place_of(x, z, 1) for x, z in planes], stretch)
+    keep(2, smooth(field, ngx, ngz, gy, per * n, emit))
+    send_all(early.at[0], earlies.at[0, place], 2, 5)
+
+    wait(back.at[0], recv_sem.at[2])
+    yf = flat(back.at[0], 0, s)
+    early[1] = pack(26.0 * dot_nt(yf, yf))
+    send_all(early.at[1], earlies.at[1, place], 3, 6)
+
+    wait(back.at[1], recv_sem.at[3])
+    zf = flat(back.at[1], 0, s)
     uf = zf - yf
-    share(1, jnp.concatenate([dot_nt(uf, uf), dot_nt(zf, q)], axis=1))
-
-    gram_zr, gram_pq = shared(0)
+    part[...] = pack(jnp.concatenate([dot_nt(uf, uf), dot_nt(zf, q)], axis=1))
+    send_all(part, parts.at[place], 4, 7)
+
+    def summed(ref):
+        return tree_sum([ref[i] for i in range(everyone)])
+
+    wait(earlies.at[0], recv_sem.at[5])
+    gram_pq = unpack(summed(earlies.at[0]), n)
+    wait(earlies.at[1], recv_sem.at[6])
+    gram_zr = unpack(summed(earlies.at[1]), n)
     beta = dot(inverse, gram_zr)
     beta_t = beta.T
     known = gram_zr + dot(beta_t, dot(gram_pq, beta))
     mixed = dot(beta_t, jnp.concatenate([p, q], axis=1))
     direction = zf + mixed[:, : s * width]
-    wait(back.at[pl.ds(0, n * s), :], recv_sem.at[4])
-    wf = flat(back, [4 * s + i for i in range(s)], stretch)
+    wait(back.at[2], recv_sem.at[4])
+    wf = flat(back.at[2], 0, s)
     both = jnp.concatenate([direction, wf + mixed[:, s * width :]], axis=1)
     for i in range(s):
         dir_out[pl.ds(i, n, stride=s), :] = direction[:, i * width : (i + 1) * width]
     loads[4].wait()
-    wait(done.at[pl.ds(0, (n - 1) * s + n), :], send_sem.at[0])
-    wait(done.at[pl.ds(0, (n - 1) * 3 * s), :], send_sem.at[1])
-    wait(parts.at[0, pl.ds(0, everyone - 1)], send_sem.at[2])
-
-    gram_uu, gram_zq = shared(1)
+    wait(land.at[pl.ds(0, (level * ngx - 1) * some), :], send_sem.at[0])
+    by_plane(lambda begin, end: wait(land.at[pl.ds(0, level * ngx * per * (end - begin)), :], send_sem.at[6]))
+    wait(halo, send_sem.at[5])
+    wait(back.at[pl.ds(0, 3), pl.ds(0, (n // per - 1) * some), :], send_sem.at[1])
+    wait(earlies.at[0, pl.ds(0, everyone - 1)], send_sem.at[2])
+    wait(earlies.at[1, pl.ds(0, everyone - 1)], send_sem.at[3])
+
+    wait(parts, recv_sem.at[7])
+    total = unpack(summed(parts), 2 * n)
+    gram_uu, gram_zq = total[:, :n], total[:, n:]
     curvature = known - 26.0 * gram_uu + dot(gram_zq, beta) + dot_nt(beta_t, gram_zq)
     alpha = eliminate(curvature, gram_zr)
     step = dot(alpha.T, both)
@@ -383,7 +485,7 @@
         rows = pl.ds(i, n, stride=s)
         sol_out[rows, :] = sol[rows, :] + step[:, i * width : (i + 1) * width]
         res_out[rows, :] = res[rows, :] - step[:, (s + i) * width : (s + i + 1) * width]
-    wait(parts.at[1, pl.ds(0, everyone - 1)], send_sem.at[3])
+    wait(parts.at[pl.ds(0, everyone - 1)], send_sem.at[4])
 
 
 def write(*refs):
@@ -405,7 +507,8 @@
     anywhere = pl.BlockSpec(memory_space=pl.ANY)
     inside = pl.BlockSpec(memory_space=pltpu.VMEM)
     block = pltpu.VMEM((rows, width), jnp.float32)
-    packed = 2 * n * n // 128
+    per = 2 * n // (ngx * ngz)
+    packed = n * n // 128
     outs = pl.pallas_call(
         functools.partial(kernel, sizes),
         out_shape=(block,) * 3,
@@ -414,16 +517,18 @@
         scratch_shapes=[
             block, block, block, block,
             pltpu.VMEM((n, n), jnp.float32),
-            block,
+            pltpu.VMEM((per * rows, width), jnp.float32),
             pltpu.VMEM((n, 1, width), jnp.float32),
-            pltpu.VMEM((n, 1, width), jnp.float32),
-            pltpu.VMEM((5 * rows, width), jnp.float32),
-            pltpu.VMEM((5 * rows, width), jnp.float32),
+            pltpu.VMEM((per * n, 1, width), jnp.float32),
+            pltpu.VMEM((3, per * rows, width), jnp.float32),
+            pltpu.VMEM((3, rows, width), jnp.float32),
+            pltpu.VMEM((2 * packed, 128), jnp.float32),
+            pltpu.VMEM((everyone, 2 * packed, 128), jnp.float32),
             pltpu.VMEM((2, packed, 128), jnp.float32),
             pltpu.VMEM((2, everyone, packed, 128), jnp.float32),
             pltpu.SemaphoreType.DMA((5,)),
-            pltpu.SemaphoreType.DMA((4,)),
             pltpu.SemaphoreType.DMA((7,)),
+            pltpu.SemaphoreType.DMA((9,)),
         ],
         compiler_params=pltpu.CompilerParams(
             collective_id=0, has_side_effects=True
@@ -445,7 +550,7 @@
     ngx, ngy, ngz = (mesh.shape[axis] for axis in ("gx", "gy", "gz"))
     n, lx, lz, width = residual.shape
     fits = n == ngx * ngz and lx % 2 == 0 and lz % 2 == 0 and (lx * lz) % 8 == 0
-    fits = fits and width % 128 == 0 and n % 16 == 0 and 128 % (2 * n) == 0 and ngy == 2 and width % (lx * lz) == 0 and width // (lx * lz) >= 15
+    fits = fits and width % 128 == 0 and n % 16 == 0 and 128 % (2 * n) == 0 and ngy == 2 and ngz > 1 and width >= 4 * (width // (lx * lz)) and (ngx & (ngx - 1)) == 0 and (ngz & (ngz - 1)) == 0 and width % (lx * lz) == 0 and width // (lx * lz) >= 15
     args = (solution, residual, direction_prev, image_prev, gram_prev)
     if fits:
         return whole_body((ngx, ngy, ngz, n, lx, lz, width), *args)

time: 24.9 us -> 23.6 us (0.948)
  Pallas kernels: 24.1 us -> 22.8 us
    pallas_call x1, Pallas kernels: 23.4 us -> 22.1 us  [whole_body(): pl.pallas_call(functools.partial(kernel, sizes), out_shape=(block,) * 3,...]
where the time goes in v2:
time: 23.6 us; the launch traced here: 23.4 us
  Pallas kernels  22.8 us (97%)
  between operations  0.64 us (3%)
    pallas_call x1, Pallas kernels, whole_body(): pl.pallas_call(functools.partial(kernel, sizes), out_shape=(block,) * 3,...  22.1 us
    pallas_call x1, Pallas kernels, whole_body(): pl.pallas_call(write, out_shape=(field,) * 3, in_specs=[inside] * 3, out_...  0.7 us

profile of v2, /device:TPU:0, one launch (start us, length us, event | category | flops | bytes accessed | tf_op | source)
XLA Modules:
  0.0 23.4 jit_solution(14409525087836038554)
XLA Ops:
  0.6 22.1 %shard_map.76 = (f32[128,128]{1,0:T(8,128)S(1)}, f32[128,128]{1,0:T(8,128)S(1)}, f32[128,128]{1,0:T(8,128)S(1)}) custom-call(f32[128,128]{1,0:T(8,128)} %bitcast.7, f32[128,128]{1,0:T(8,128)} %bitcast.8, f32[128,128]{1,0:T(8,128)} %bitcast.9, f32[128,128]{1,0:T(8,128)} %bitcast.10, f32[16,16]{1,0:T(8,128)} %gram_in.1), custom_call_target="tpu_custom_call" | custom-call | tf_op jit(solution)/shard_map/pallas_call | solution.py:512
  22.7 0.7 %shard_map.77 = (f32[128,128]{1,0:T(8,128)}, f32[128,128]{1,0:T(8,128)}, f32[128,128]{1,0:T(8,128)}) custom-call(f32[128,128]{1,0:T(8,128)S(1)} %get-tuple-element.9.refs_0_, f32[128,128]{1,0:T(8,128)S(1)} %get-tuple-element.10.refs_1_, f32[128,128]{1,0:T(8,128)S(1)} %get-tuple-element.11.refs_2_), custom_call_target="tpu_custom_call" | custom-call | tf_op jit(solution)/shard_map/pallas_call | solution.py:538

commit v3 on v2

--- a/solution.py
+++ b/solution.py
@@ -113,6 +113,41 @@
     )
 
 
+def parts_of(value):
+    first = value.astype(jnp.bfloat16)
+    rest = value - first.astype(jnp.float32)
+    second = rest.astype(jnp.bfloat16)
+    third = (rest - second.astype(jnp.float32)).astype(jnp.bfloat16)
+    return first, second, third
+
+
+def product(left, right, contract):
+    order = left[0].shape[0]
+    total = None
+    for i, term in enumerate(right):
+        stack = jnp.concatenate(left[: 3 - i], axis=0) if i < 2 else left[0]
+        out = lax.dot_general(stack, term, (contract, ((), ())), preferred_element_type=jnp.float32)
+        for j in range(3 - i):
+            piece = out[j * order : (j + 1) * order]
+            total = piece if total is None else total + piece
+    return total
+
+
+def gram_of(left, right):
+    return product(left, right, ((1,), (1,)))
+
+
+def small(left, right):
+    return product(parts_of(left), parts_of(right), ((1,), (0,)))
+
+
+def wide(turned, right):
+    a, b, c = (v.astype(jnp.float32) for v in parts_of(turned))
+    d, e, f = right
+    left = jnp.concatenate([a, a, b, b, a, c], axis=0).T.astype(jnp.bfloat16)
+    return jnp.dot(left, jnp.concatenate([d, e, d, e, f, d], axis=0), preferred_element_type=jnp.float32)
+
+
 def eliminate(matrix, target):
     order = matrix.shape[0]
     rows = lax.broadcasted_iota(jnp.int32, matrix.shape, 0)
@@ -129,27 +164,29 @@
     return target * scale
 
 
-def smooth(res, ngx, ngz, gy, whole, emit):
+def smooth(res, ngx, ngz, gy, ends):
     lx, lz = len(res), len(res[0])
     count, ny = res[0][0].shape
     row = lax.broadcasted_iota(jnp.int32, (count, ny), 0)
     lane = lax.broadcasted_iota(jnp.int32, (count, ny), 1)
     even = lane % 2 == 0
-    inner = row % (ngx * ngz)
     edges = {
-        "xp": (inner < ngz, ngz),
-        "xn": (inner >= (ngx - 1) * ngz, count - ngz),
+        "xp": (row < ngz, ngz),
+        "xn": (row >= (ngx - 1) * ngz, count - ngz),
         "zp": (row % ngz == 0, 1),
         "zn": (row % ngz == ngz - 1, count - 1),
     }
-    first = jnp.where(jnp.logical_and(row < whole, gy == 0), 0, -8)
-    last = jnp.where(jnp.logical_and(row < whole, gy != 0), ny - 1, -8)
-    cut = jnp.where(row < whole, jnp.where(gy == 0, ny - 3, 0), -8)
-    valid = jnp.logical_or(lane < cut, lane > cut + 2)
-    valid_even, valid_odd = jnp.logical_and(valid, even), jnp.logical_and(valid, jnp.logical_not(even))
-    twice = 2.0 - jnp.where(lane == first, 1.0, 0.0) - jnp.where(lane == last, 1.0, 0.0)
-    below = 3.0 - jnp.where(lane == first + 1, 1.0, 0.0) - jnp.where(lane == last, 1.0, 0.0)
-    above = 3.0 - jnp.where(lane == last - 1, 1.0, 0.0) - jnp.where(lane == first, 1.0, 0.0)
+    odd = jnp.logical_not(even)
+    if ends:
+        first, last = jnp.where(gy == 0, 0, -8), jnp.where(gy == 0, -8, ny - 1)
+        cut = jnp.where(gy == 0, ny - 3, 0)
+        valid = jnp.logical_or(lane < cut, lane > cut + 2)
+        valid_even, valid_odd = jnp.logical_and(valid, even), jnp.logical_and(valid, odd)
+        twice = 2.0 - jnp.where(jnp.logical_or(lane == first, lane == last), 1.0, 0.0)
+        below = 3.0 - jnp.where(jnp.logical_or(lane == first + 1, lane == last), 1.0, 0.0)
+        above = 3.0 - jnp.where(jnp.logical_or(lane == last - 1, lane == first), 1.0, 0.0)
+    else:
+        twice, below, above = jnp.float32(2.0), jnp.float32(3.0), jnp.float32(3.0)
     zero = jnp.zeros((count, ny), jnp.float32)
     memo = {}
 
@@ -188,6 +225,8 @@
         return moved(add(state[x, z], z_pair(x, z)), kind)
 
     def woven(at_even, at_odd):
+        if not ends:
+            return jnp.where(even, at_even, at_odd)
         return jnp.where(valid_even, at_even, jnp.where(valid_odd, at_odd, zero))
 
     def shifted(value, k):
@@ -229,13 +268,13 @@
                     base = both + once(mix)
                     fresh[x, z] = third * jnp.where(even, base + third * two(mix), base)
         state.update(fresh)
-        emit(step, forward, state)
+        yield forward, state
     image = {}
     for x in range(lx):
         for z in range(lz):
             box = add(state[x, z], neighbours(x, z))
-            image[x, z] = 27.0 * state[x, z] - (box + once(jnp.where(valid, box, zero)))
-    return image
+            image[x, z] = 27.0 * state[x, z] - (box + once(jnp.where(valid, box, zero) if ends else box))
+    yield image, None
 
 
 def pack(value):
@@ -379,7 +418,8 @@
     for load in loads[1:4]:
         load.wait()
     p, q = flat(prev, 0, s), flat(prev_img, 0, s)
-    early[0] = pack(dot_nt(p, q))
+    q_parts = parts_of(q)
+    early[0] = pack(gram_of(parts_of(p), q_parts))
     eye = (lax.broadcasted_iota(jnp.int32, (n, n), 0) == lax.broadcasted_iota(jnp.int32, (n, n), 1)).astype(jnp.float32)
     inverse = eliminate(0.5 * (gram[...] + gram[...].T), eye)
 
@@ -395,76 +435,98 @@
     def _():
         wait(land.at[pl.ds(0, below), :], recv_sem.at[8])
 
+
+    lines = {(x, z): [land[pl.ds(a * s + x * lz + z, n, stride=some), :] for a in range(per)] for x, z in planes}
+    sweeps = [
+        smooth([[lines[x, z][a] for z in range(lz)] for x in range(lx)], ngx, ngz, gy, True) for a in range(per)
+    ]
+    begun = [[next(sweep) for _ in range(2)] for sweep in sweeps]
     wait(halo, recv_sem.at[1])
     beyond = [jnp.concatenate([halo[i * per + a] for i in range(n)], axis=0) for a in range(per)]
     zone = width // per
     outer = jnp.where(gy == 0, zone - depth, 0)
     shift = jnp.where(gy == 0, zone, depth)
 
-    def extended(i):
-        lines = [land[pl.ds(a * s + i, n, stride=some), :] for a in range(per)]
+    def border_of(x, z):
+        i = x * lz + z
         edge = None
         for a in range(per):
             begin = a * zone
-            inside = pltpu.roll(lines[a], lax.rem(begin + shift + jnp.where(gy == 0, width - depth, 0), width), 1)
+            inside = pltpu.roll(lines[x, z][a], lax.rem(begin + shift + jnp.where(gy == 0, width - depth, 0), width), 1)
             outside = pltpu.roll(beyond[a], lax.rem(begin + outer + width - i * depth, width), 1)
             at = lanes - (begin + outer)
             value = jnp.where(jnp.logical_and(at >= 0, at < depth), outside, inside)
             edge = value if edge is None else jnp.where(lanes >= begin, value, edge)
-        return jnp.concatenate(lines + [edge], axis=0)
+        return edge
 
     border = jnp.where(gy == 0, width - depth, 0)
     at_border = jnp.logical_and(lanes >= border, lanes < border + depth)
 
-    def keep(field, values):
+    def keep(field, values, odd=None):
         for i, (x, z) in enumerate(planes):
-            edge = values[x, z][per * n :]
+            if odd is not None and x % 2 != odd:
+                continue
+            edge = values[per][x, z]
             for a in range(per):
                 back_shift = lax.rem(2 * width - a * zone - shift - jnp.where(gy == 0, width - depth, 0), width)
-                value = jnp.where(at_border, pltpu.roll(edge, back_shift, 1), values[x, z][a * n : (a + 1) * n])
+                value = jnp.where(at_border, pltpu.roll(edge, back_shift, 1), values[a][x, z])
                 done[field, pl.ds(a * s + i, n, stride=some), :] = value
-        target = back.at[field, pl.ds(owner * some, some), :]
+        source, target = (ref.at[field].reshape(ref.shape[1] // s, s, width) for ref in (done, back))
+        rows = pl.ds(0, s) if odd is None else pl.ds(odd * (s // 2), s // 2)
+        target = target.at[pl.ds(owner * per, per), rows, :]
         for same, level_with, _, home, where in flock:
             if same and level_with:
-                remote(done.at[field, pl.ds(home * some, some), :], target, 1, 2 + field, where)
-        pltpu.make_async_copy(done.at[field, pl.ds(column * some, some), :], target, recv_sem.at[2 + field]).start()
-
-    def emit(step, forward, state):
-        if step == 3:
-            keep(0, forward)
-        if step == 6:
-            keep(1, state)
-
-    field = [[extended(x * lz + z) for z in range(lz)] for x in range(lx)]
-    keep(2, smooth(field, ngx, ngz, gy, per * n, emit))
+                remote(source.at[pl.ds(home * per, per), rows, :], target, 1, 2 + field, where)
+        pltpu.make_async_copy(source.at[pl.ds(column * per, per), rows, :], target, recv_sem.at[2 + field]).start()
+
+    edge_rows = [[border_of(x, z) for z in range(lz)] for x in range(lx)]
+    sweeps.append(smooth(edge_rows, ngx, ngz, gy, False))
+    begun.append([])
+    for step in range(8):
+        found = [past[step] if step < len(past) else next(sweep) for past, sweep in zip(begun, sweeps)]
+        if step in (1, 3):
+            keep(0, [forward for forward, _ in found], step // 2)
+        if step in (4, 6):
+            keep(1, [state for _, state in found], 1 if step == 4 else 0)
+    keep(2, [image for image, _ in found])
     send_all(early.at[0], earlies.at[0, place], 2, 5)
 
     wait(back.at[0], recv_sem.at[2])
     yf = flat(back.at[0], 0, s)
-    early[1] = pack(26.0 * dot_nt(yf, yf))
+    y_parts = parts_of(yf)
+    early[1] = pack(26.0 * gram_of(y_parts, y_parts))
     send_all(early.at[1], earlies.at[1, place], 3, 6)
 
     wait(back.at[1], recv_sem.at[3])
     zf = flat(back.at[1], 0, s)
     uf = zf - yf
-    part[...] = pack(jnp.concatenate([dot_nt(uf, uf), dot_nt(zf, q)], axis=1))
+    u_parts = parts_of(uf)
+    part[...] = pack(jnp.concatenate([gram_of(u_parts, u_parts), gram_of(parts_of(zf), q_parts)], axis=1))
     send_all(part, parts.at[place], 4, 7)
 
     def summed(ref):
         return tree_sum([ref[i] for i in range(everyone)])
 
     wait(earlies.at[0], recv_sem.at[5])
-    gram_pq = unpack(summed(earlies.at[0]), n)
+    middle = dot(dot(inverse, unpack(summed(earlies.at[0]), n)), inverse)
+    pair_parts = parts_of(jnp.concatenate([inverse, middle], axis=0))
     wait(earlies.at[1], recv_sem.at[6])
     gram_zr = unpack(summed(earlies.at[1]), n)
-    beta = dot(inverse, gram_zr)
-    beta_t = beta.T
-    known = gram_zr + dot(beta_t, dot(gram_pq, beta))
-    mixed = dot(beta_t, jnp.concatenate([p, q], axis=1))
+    zr_parts = parts_of(gram_zr)
+    found = product(pair_parts, zr_parts, ((1,), (0,)))
+    beta, inner = found[:n], found[n:]
+    known = gram_zr + product(zr_parts, parts_of(inner), ((1,), (0,)))
+    blocks = 128 // (2 * n)
+    right_parts = parts_of(jnp.concatenate([-26.0 * eye, beta] * blocks, axis=0))
+    left_parts = parts_of(jnp.concatenate([0.0 * eye, beta] * blocks, axis=0).T)
+    row, lane = (lax.broadcasted_iota(jnp.int32, (n, 128), i) for i in range(2))
+    mine_only = row // (n // blocks) == lane // (2 * n)
+    mixed = wide(beta, parts_of(jnp.concatenate([p, q], axis=1)))
     direction = zf + mixed[:, : s * width]
     wait(back.at[2], recv_sem.at[4])
     wf = flat(back.at[2], 0, s)
     both = jnp.concatenate([direction, wf + mixed[:, s * width :]], axis=1)
+    both_parts = parts_of(both)
     for i in range(s):
         dir_out[pl.ds(i, n, stride=s), :] = direction[:, i * width : (i + 1) * width]
     loads[4].wait()
@@ -476,11 +538,10 @@
     wait(earlies.at[1, pl.ds(0, everyone - 1)], send_sem.at[3])
 
     wait(parts, recv_sem.at[7])
-    total = unpack(summed(parts), 2 * n)
-    gram_uu, gram_zq = total[:, :n], total[:, n:]
-    curvature = known - 26.0 * gram_uu + dot(gram_zq, beta) + dot_nt(beta_t, gram_zq)
+    total = parts_of(jnp.where(mine_only, jnp.concatenate([summed(parts)] * blocks, axis=0), 0.0))
+    curvature = known + product(total, right_parts, ((1,), (0,))) + gram_of(left_parts, total)
     alpha = eliminate(curvature, gram_zr)
-    step = dot(alpha.T, both)
+    step = wide(alpha, both_parts)
     for i in range(s):
         rows = pl.ds(i, n, stride=s)
         sol_out[rows, :] = sol[rows, :] + step[:, i * width : (i + 1) * width]
@@ -549,7 +610,7 @@
 def pick_body(mesh, solution, residual, direction_prev, image_prev, gram_prev):
     ngx, ngy, ngz = (mesh.shape[axis] for axis in ("gx", "gy", "gz"))
     n, lx, lz, width = residual.shape
-    fits = n == ngx * ngz and lx % 2 == 0 and lz % 2 == 0 and (lx * lz) % 8 == 0
+    fits = n == ngx * ngz and lx == 2 and lz % 2 == 0 and (lx * lz) % 8 == 0
     fits = fits and width % 128 == 0 and n % 16 == 0 and 128 % (2 * n) == 0 and ngy == 2 and ngz > 1 and width >= 4 * (width // (lx * lz)) and (ngx & (ngx - 1)) == 0 and (ngz & (ngz - 1)) == 0 and width % (lx * lz) == 0 and width // (lx * lz) >= 15
     args = (solution, residual, direction_prev, image_prev, gram_prev)
     if fits:

time: 23.6 us -> 22.9 us (0.970)
  Pallas kernels: 22.8 us -> 22.1 us
    pallas_call x1, Pallas kernels: 22.1 us -> 21.4 us  [whole_body(): pl.pallas_call(functools.partial(kernel, sizes), out_shape=(block,) * 3,...]
where the time goes in v3:
time: 22.9 us; the launch traced here: 22.8 us
  Pallas kernels  22.1 us (97%)
  between operations  0.64 us (3%)
    pallas_call x1, Pallas kernels, whole_body(): pl.pallas_call(functools.partial(kernel, sizes), out_shape=(block,) * 3,...  21.4 us
    pallas_call x1, Pallas kernels, whole_body(): pl.pallas_call(write, out_shape=(field,) * 3, in_specs=[inside] * 3, out_...  0.7 us

profile of v3, /device:TPU:0, one launch (start us, length us, event | category | flops | bytes accessed | tf_op | source)
XLA Modules:
  0.0 22.8 jit_solution(17290919538210754428)
XLA Ops:
  0.6 21.4 %shard_map.76 = (f32[128,128]{1,0:T(8,128)S(1)}, f32[128,128]{1,0:T(8,128)S(1)}, f32[128,128]{1,0:T(8,128)S(1)}) custom-call(f32[128,128]{1,0:T(8,128)} %bitcast.7, f32[128,128]{1,0:T(8,128)} %bitcast.8, f32[128,128]{1,0:T(8,128)} %bitcast.9, f32[128,128]{1,0:T(8,128)} %bitcast.10, f32[16,16]{1,0:T(8,128)} %gram_in.1), custom_call_target="tpu_custom_call" | custom-call | tf_op jit(solution)/shard_map/pallas_call | solution.py:573
  22.1 0.7 %shard_map.77 = (f32[128,128]{1,0:T(8,128)}, f32[128,128]{1,0:T(8,128)}, f32[128,128]{1,0:T(8,128)}) custom-call(f32[128,128]{1,0:T(8,128)S(1)} %get-tuple-element.9.refs_0_, f32[128,128]{1,0:T(8,128)S(1)} %get-tuple-element.10.refs_1_, f32[128,128]{1,0:T(8,128)S(1)} %get-tuple-element.11.refs_2_), custom_call_target="tpu_custom_call" | custom-call | tf_op jit(solution)/shard_map/pallas_call | solution.py:599

commit v4 on v3

--- a/solution.py
+++ b/solution.py
@@ -338,17 +338,20 @@
         )
         for k in range(ngz - 1)
     ] + [gz]
-    across = [jnp.bitwise_xor(gx, dx) for dx in range(ngx)]
+    chip = gx - jnp.bitwise_and(gx, 1)
+    across = [jnp.bitwise_xor(chip, dx) for dx in range(ngx)]
     ways = sorted(
         ((dx, dy, k) for dx in range(ngx) for dy in range(ngy) for k in range(ngz)),
-        key=lambda way: (way[2] >= level, way[2] - (way[0] > 1) - way[1], -way[1], -way[0]),
+        key=lambda way: (way[2] >= level, way[0] % 2, -way[1], way[2] - (way[0] > 1)),
     )
     flock = []
     for dx, dy, k in ways:
         if (dx, dy, k) != (0, 0, ngz - 1):
             ox, oy, oz = across[dx], 1 - gy if dy else gy, floors[k]
-            owner = ox * level + jnp.bitwise_and(oz, level - 1)
-            flock.append((dy == 0, k >= level, owner, ox * ngz + oz, {"gx": ox, "gy": oy, "gz": oz}))
+            if (dx, dy, k) == (1, 0, ngz - 1):
+                ox = jnp.bitwise_xor(gx, 1)
+            into = ox * level + jnp.bitwise_and(oz, level - 1)
+            flock.append((dy == 0, k >= level, into, ox * ngz + oz, {"gx": ox, "gy": oy, "gz": oz}))
     owner = gx * level + jnp.bitwise_and(gz, level - 1)
 
     def remote(source, target, sent, arrived, where):

time: 22.9 us -> 22.4 us (0.978)
  Pallas kernels: 22.1 us -> 21.6 us
    pallas_call x1, Pallas kernels: 21.4 us -> 20.9 us  [whole_body(): pl.pallas_call(functools.partial(kernel, sizes), out_shape=(block,) * 3,...]
where the time goes in v4:
time: 22.4 us; the launch traced here: 22.2 us
  Pallas kernels  21.6 us (96%)
  between operations  0.64 us (3%)
    pallas_call x1, Pallas kernels, whole_body(): pl.pallas_call(functools.partial(kernel, sizes), out_shape=(block,) * 3,...  20.9 us
    pallas_call x1, Pallas kernels, whole_body(): pl.pallas_call(write, out_shape=(field,) * 3, in_specs=[inside] * 3, out_...  0.7 us

profile of v4, /device:TPU:0, one launch (start us, length us, event | category | flops | bytes accessed | tf_op | source)
XLA Modules:
  0.0 22.2 jit_solution(14787133963432048463)
XLA Ops:
  0.6 20.9 %shard_map.76 = (f32[128,128]{1,0:T(8,128)S(1)}, f32[128,128]{1,0:T(8,128)S(1)}, f32[128,128]{1,0:T(8,128)S(1)}) custom-call(f32[128,128]{1,0:T(8,128)} %bitcast.7, f32[128,128]{1,0:T(8,128)} %bitcast.8, f32[128,128]{1,0:T(8,128)} %bitcast.9, f32[128,128]{1,0:T(8,128)} %bitcast.10, f32[16,16]{1,0:T(8,128)} %gram_in.1), custom_call_target="tpu_custom_call" | custom-call | tf_op jit(solution)/shard_map/pallas_call | solution.py:576
  21.5 0.7 %shard_map.77 = (f32[128,128]{1,0:T(8,128)}, f32[128,128]{1,0:T(8,128)}, f32[128,128]{1,0:T(8,128)}) custom-call(f32[128,128]{1,0:T(8,128)S(1)} %get-tuple-element.9.refs_0_, f32[128,128]{1,0:T(8,128)S(1)} %get-tuple-element.10.refs_1_, f32[128,128]{1,0:T(8,128)S(1)} %get-tuple-element.11.refs_2_), custom_call_target="tpu_custom_call" | custom-call | tf_op jit(solution)/shard_map/pallas_call | solution.py:602

commit v5 on v4

--- a/solution.py
+++ b/solution.py
@@ -344,9 +344,10 @@
         ((dx, dy, k) for dx in range(ngx) for dy in range(ngy) for k in range(ngz)),
         key=lambda way: (way[2] >= level, way[0] % 2, -way[1], way[2] - (way[0] > 1)),
     )
+    ways.remove((0, 0, ngz - 1))
     flock = []
     for dx, dy, k in ways:
-        if (dx, dy, k) != (0, 0, ngz - 1):
+        if True:
             ox, oy, oz = across[dx], 1 - gy if dy else gy, floors[k]
             if (dx, dy, k) == (1, 0, ngz - 1):
                 ox = jnp.bitwise_xor(gx, 1)
@@ -365,7 +366,7 @@
 
     land[...] = jnp.zeros_like(land)
     barrier = pltpu.get_barrier_semaphore()
-    for peer in flock:
+    for _, peer in sorted(zip(ways, flock), key=lambda pair: pair[0][2] - (pair[0][0] > 1) - pair[0][1]):
         pl.semaphore_signal(barrier, inc=1, device_id=peer[4], device_id_type=MESH)
     loads[0].wait()
     depth = width // s
@@ -387,26 +388,26 @@
             here = functools.reduce(jnp.logical_or, [gz == g for g in range(ngz) if spans[g] == span])
             pl.when(here)(functools.partial(work, *span))
 
+    def edge(into, where):
+        remote(strip.at[pl.ds(into * per, per)], halo.at[pl.ds(column * per, per)], 5, 1, where)
+
     def cross(begin, end):
         for same, level_with, into, _, where in flock:
-            if same and not level_with:
+            if not level_with and not same:
+                edge(into, where)
+            elif not level_with:
                 remote(
                     res.reshape(n, s, width).at[pl.ds(into * per, per), pl.ds(begin, end - begin), :],
                     land.reshape(per * n, s, width).at[pl.ds(column * per, per), pl.ds(begin, end - begin), :],
                     6, 8, where,
                 )
 
-    def edges(level_with_me):
-        for same, level_with, into, _, where in flock:
-            if not same and level_with == level_with_me:
-                remote(strip.at[pl.ds(into * per, per)], halo.at[pl.ds(column * per, per)], 5, 1, where)
-
-    edges(False)
     by_plane(cross)
-    edges(True)
     for same, level_with, into, _, where in flock:
-        if same and level_with:
+        if level_with and same:
             remote(res.at[pl.ds(into * some, some), :], mine, 0, 0, where)
+        elif level_with:
+            edge(into, where)
     pltpu.make_async_copy(res.at[pl.ds(owner * some, some), :], mine, recv_sem.at[0]).start()
 
     def flat(ref, first, stride):
@@ -553,13 +554,11 @@
 
 
 def write(*refs):
-    half = len(refs) // 2
-    semaphore = refs[-1]
-    stores = [pltpu.make_async_copy(refs[i], refs[half + i], semaphore.at[i]) for i in range(half)]
-    for store in stores:
-        store.start()
-    for store in stores:
-        store.wait()
+    *arrays, size, semaphore = refs
+    half = len(arrays) // 2
+    for source, target in zip(arrays[:half], arrays[half:]):
+        pltpu.make_async_copy(source, target, semaphore).start()
+    pltpu.make_async_copy(size, size, semaphore).wait()
 
 
 def whole_body(sizes, *args):
@@ -604,7 +603,7 @@
         out_shape=(field,) * 3,
         in_specs=[inside] * 3,
         out_specs=[anywhere] * 3,
-        scratch_shapes=[pltpu.SemaphoreType.DMA((3,))],
+        scratch_shapes=[pltpu.VMEM((3 * rows, width), jnp.float32), pltpu.SemaphoreType.DMA],
 
     )(*outs)
     return tuple(a.reshape(shape) for a in outs)

time: 22.4 us -> 22.3 us (level)
  no operation moved by 1% of the time
where the time goes in v5:
time: 22.3 us; the launch traced here: 22.2 us
  Pallas kernels  21.5 us (96%)
  between operations  0.64 us (3%)
    pallas_call x1, Pallas kernels, whole_body(): pl.pallas_call(functools.partial(kernel, sizes), out_shape=(block,) * 3,...  20.9 us
    pallas_call x1, Pallas kernels, whole_body(): pl.pallas_call(write, out_shape=(field,) * 3, in_specs=[inside] * 3, out_...  0.68 us

profile of v5, /device:TPU:0, one launch (start us, length us, event | category | flops | bytes accessed | tf_op | source)
XLA Modules:
  0.0 22.2 jit_solution(6663023944356249657)
XLA Ops:
  0.6 20.9 %shard_map.76 = (f32[128,128]{1,0:T(8,128)S(1)}, f32[128,128]{1,0:T(8,128)S(1)}, f32[128,128]{1,0:T(8,128)S(1)}) custom-call(f32[128,128]{1,0:T(8,128)} %bitcast.7, f32[128,128]{1,0:T(8,128)} %bitcast.8, f32[128,128]{1,0:T(8,128)} %bitcast.9, f32[128,128]{1,0:T(8,128)} %bitcast.10, f32[16,16]{1,0:T(8,128)} %gram_in.1), custom_call_target="tpu_custom_call" | custom-call | tf_op jit(solution)/shard_map/pallas_call | solution.py:575
  21.5 0.7 %shard_map.77 = (f32[128,128]{1,0:T(8,128)}, f32[128,128]{1,0:T(8,128)}, f32[128,128]{1,0:T(8,128)}) custom-call(f32[128,128]{1,0:T(8,128)S(1)} %get-tuple-element.9.refs_0_, f32[128,128]{1,0:T(8,128)S(1)} %get-tuple-element.10.refs_1_, f32[128,128]{1,0:T(8,128)S(1)} %get-tuple-element.11.refs_2_), custom_call_target="tpu_custom_call" | custom-call | tf_op jit(solution)/shard_map/pallas_call | solution.py:601

commit v6 on v5

--- a/solution.py
+++ b/solution.py
@@ -389,7 +389,7 @@
             pl.when(here)(functools.partial(work, *span))
 
     def edge(into, where):
-        remote(strip.at[pl.ds(into * per, per)], halo.at[pl.ds(column * per, per)], 5, 1, where)
+        remote(strip.at[pl.ds(into * per, per)], halo.at[pl.ds(column * per, per)], 0, 1, where)
 
     def cross(begin, end):
         for same, level_with, into, _, where in flock:
@@ -399,7 +399,7 @@
                 remote(
                     res.reshape(n, s, width).at[pl.ds(into * per, per), pl.ds(begin, end - begin), :],
                     land.reshape(per * n, s, width).at[pl.ds(column * per, per), pl.ds(begin, end - begin), :],
-                    6, 8, where,
+                    1, 8, where,
                 )
 
     by_plane(cross)
@@ -480,7 +480,7 @@
         target = target.at[pl.ds(owner * per, per), rows, :]
         for same, level_with, _, home, where in flock:
             if same and level_with:
-                remote(source.at[pl.ds(home * per, per), rows, :], target, 1, 2 + field, where)
+                remote(source.at[pl.ds(home * per, per), rows, :], target, 0, 2 + field, where)
         pltpu.make_async_copy(source.at[pl.ds(column * per, per), rows, :], target, recv_sem.at[2 + field]).start()
 
     edge_rows = [[border_of(x, z) for z in range(lz)] for x in range(lx)]
@@ -499,14 +499,14 @@
     yf = flat(back.at[0], 0, s)
     y_parts = parts_of(yf)
     early[1] = pack(26.0 * gram_of(y_parts, y_parts))
-    send_all(early.at[1], earlies.at[1, place], 3, 6)
+    send_all(early.at[1], earlies.at[1, place], 2, 6)
 
     wait(back.at[1], recv_sem.at[3])
     zf = flat(back.at[1], 0, s)
     uf = zf - yf
     u_parts = parts_of(uf)
     part[...] = pack(jnp.concatenate([gram_of(u_parts, u_parts), gram_of(parts_of(zf), q_parts)], axis=1))
-    send_all(part, parts.at[place], 4, 7)
+    send_all(part, parts.at[place], 3, 7)
 
     def summed(ref):
         return tree_sum([ref[i] for i in range(everyone)])
@@ -534,12 +534,10 @@
     for i in range(s):
         dir_out[pl.ds(i, n, stride=s), :] = direction[:, i * width : (i + 1) * width]
     loads[4].wait()
-    wait(land.at[pl.ds(0, (level * ngx - 1) * some), :], send_sem.at[0])
-    by_plane(lambda begin, end: wait(land.at[pl.ds(0, level * ngx * per * (end - begin)), :], send_sem.at[6]))
-    wait(halo, send_sem.at[5])
-    wait(back.at[pl.ds(0, 3), pl.ds(0, (n // per - 1) * some), :], send_sem.at[1])
-    wait(earlies.at[0, pl.ds(0, everyone - 1)], send_sem.at[2])
-    wait(earlies.at[1, pl.ds(0, everyone - 1)], send_sem.at[3])
+    gone = (level * ngx - 1) * some + per * n + 3 * (n // per - 1) * some
+    wait(done.reshape(3 * n * some, width).at[pl.ds(0, gone), :], send_sem.at[0])
+    by_plane(lambda begin, end: wait(land.at[pl.ds(0, level * ngx * per * (end - begin)), :], send_sem.at[1]))
+    wait(earlies.at[pl.ds(0, 2), pl.ds(0, everyone - 1)], send_sem.at[2])
 
     wait(parts, recv_sem.at[7])
     total = parts_of(jnp.where(mine_only, jnp.concatenate([summed(parts)] * blocks, axis=0), 0.0))
@@ -550,7 +548,7 @@
         rows = pl.ds(i, n, stride=s)
         sol_out[rows, :] = sol[rows, :] + step[:, i * width : (i + 1) * width]
         res_out[rows, :] = res[rows, :] - step[:, (s + i) * width : (s + i + 1) * width]
-    wait(parts.at[pl.ds(0, everyone - 1)], send_sem.at[4])
+    wait(parts.at[pl.ds(0, everyone - 1)], send_sem.at[3])
 
 
 def write(*refs):
@@ -590,7 +588,7 @@
             pltpu.VMEM((2, packed, 128), jnp.float32),
             pltpu.VMEM((2, everyone, packed, 128), jnp.float32),
             pltpu.SemaphoreType.DMA((5,)),
-            pltpu.SemaphoreType.DMA((7,)),
+            pltpu.SemaphoreType.DMA((4,)),
             pltpu.SemaphoreType.DMA((9,)),
         ],
         compiler_params=pltpu.CompilerParams(

time: 22.3 us -> 22.3 us (level)
  no operation moved by 1% of the time
where the time goes in v6:
time: 22.3 us; the launch traced here: 22.2 us
  Pallas kernels  21.5 us (96%)
  between operations  0.64 us (3%)
    pallas_call x1, Pallas kernels, whole_body(): pl.pallas_call(functools.partial(kernel, sizes), out_shape=(block,) * 3,...  20.8 us
    pallas_call x1, Pallas kernels, whole_body(): pl.pallas_call(write, out_shape=(field,) * 3, in_specs=[inside] * 3, out_...  0.68 us

profile of v6, /device:TPU:0, one launch (start us, length us, event | category | flops | bytes accessed | tf_op | source)
XLA Modules:
  0.0 22.2 jit_solution(10466385566125092648)
XLA Ops:
  0.6 20.8 %shard_map.76 = (f32[128,128]{1,0:T(8,128)S(1)}, f32[128,128]{1,0:T(8,128)S(1)}, f32[128,128]{1,0:T(8,128)S(1)}) custom-call(f32[128,128]{1,0:T(8,128)} %bitcast.7, f32[128,128]{1,0:T(8,128)} %bitcast.8, f32[128,128]{1,0:T(8,128)} %bitcast.9, f32[128,128]{1,0:T(8,128)} %bitcast.10, f32[16,16]{1,0:T(8,128)} %gram_in.1), custom_call_target="tpu_custom_call" | custom-call | tf_op jit(solution)/shard_map/pallas_call | solution.py:573
  21.5 0.7 %shard_map.77 = (f32[128,128]{1,0:T(8,128)}, f32[128,128]{1,0:T(8,128)}, f32[128,128]{1,0:T(8,128)}) custom-call(f32[128,128]{1,0:T(8,128)S(1)} %get-tuple-element.9.refs_0_, f32[128,128]{1,0:T(8,128)S(1)} %get-tuple-element.10.refs_1_, f32[128,128]{1,0:T(8,128)S(1)} %get-tuple-element.11.refs_2_), custom_call_target="tpu_custom_call" | custom-call | tf_op jit(solution)/shard_map/pallas_call | solution.py:599
